TPU v7x, 32 devices: a whole 2x2x4 slice. The times are simulated.
32 devices in a mesh: scene: 2 (over y), tile: 4 (over z), half: 2 (over x), band: 2 (over core).
Axes of the slice: x: 2, y: 2, z: 4, core: 2. Of those that a mesh axis runs over, the one named last changes fastest.
Arguments:
- optical: bfloat16 [16, 2, 512, 512], P(('scene', 'tile'), 'band', 'half'), parts along dimension 0, may hold values from -64 to 64
- sar: bfloat16 [2, 8192, 512], P('band', ('scene', 'tile', 'half')), parts along dimension 1, may hold values from -64 to 64
- destination: int32 [128], P('scene'), parts along dimension 0, may hold values from 0 to 63, as said below
- peaks: int32 [16, 2, 8], P(('scene', 'tile', 'band')), parts along dimension 0, may hold values from 0 to 511
Outputs:
- surface: float32 [16, 512, 512], P(('scene', 'tile', 'band'), 'half'), parts along dimension 0
- peak_values: float32 [16, 8], P(('scene', 'tile', 'band')), parts along dimension 0
There are 2 independent parts, one for each index of `scene`. A program takes and returns all parts, laid end to end along the dimension named above; each array names one. Nothing has to cross between parts.
Inputs may be any that keep to these rules, and one draw needn't show every extreme that they name: destination holds every block position 0 to 63 once; the 8 blocks that start at each multiple of 8 are sent one into each run of 8 positions that starts at a multiple of 8.
All inputs are finite; a program needn't handle non-finite values.
Results may differ from a plain program's by a relative error of at most 0.014.
Values may be sent and summed in bfloat16 or wider, within the bound.
A program may use at most 64 MiB of HBM per device.

v0:
```python
import functools
import math

import jax
import jax.numpy as jnp
import numpy as np
from jax import lax
from jax.experimental import pallas as pl
from jax.experimental.pallas import tpu as pltpu
from jax.sharding import PartitionSpec as P

MESH = pl.DeviceIdType.MESH

precise = lax.Precision.HIGHEST
EPSILON = 1e-06


def fourier_tables(extent):
    places = jnp.arange(extent, dtype=jnp.int32)
    phases = places[:, None] * places[None, :] % extent
    angles = phases.astype(jnp.float32) * (2.0 * math.pi / extent)
    return (jnp.cos(angles), jnp.sin(angles))


def fourier_pair(table):
    upper = table.astype(jnp.bfloat16)
    lower = (table - upper.astype(jnp.float32)).astype(jnp.bfloat16)
    return (upper, lower)


def column_spectrum(samples, table_upper, table_lower):
    extent = samples.shape[-1]
    values = samples.reshape(-1, extent)
    spectrum = jnp.dot(values, table_upper, preferred_element_type=jnp.float32) + jnp.dot(
        values, table_lower, preferred_element_type=jnp.float32
    )
    return spectrum.astype(jnp.bfloat16).reshape(samples.shape[:-1] + (2 * extent,))


def row_spectrum(columns, table_upper, table_lower):
    line_count = columns.shape[-3]
    stacked = jnp.concatenate([columns[..., 0, :], columns[..., 1, :]], axis=-2)
    result = jnp.einsum("kr,...rc->...kc", table_upper, stacked, preferred_element_type=jnp.float32)
    result = result + jnp.einsum(
        "kr,...rc->...kc", table_lower, stacked, preferred_element_type=jnp.float32
    )
    return (result[..., :line_count, :], result[..., line_count:, :])


def relay_blocks(parcel):
    layout = parcel.shape
    merged = parcel.reshape(layout[:1] + (layout[1] * layout[2],) + layout[3:])
    arrived = lax.all_to_all(merged, ("tile", "half"), split_axis=1, concat_axis=1, tiled=True)
    return arrived.reshape(layout)


def generic(optical, sar, destination, peaks):
    tile_count = lax.axis_size("tile")
    half_count = lax.axis_size("half")
    band_count = lax.axis_size("band")
    group_size = tile_count * half_count
    patch_dev, local_bands, quarter, extent = optical.shape
    col_width = extent // half_count
    block_lines = sar.shape[1] // group_size
    band_total = local_bands * band_count
    pixel_count = extent * extent
    patch_total = patch_dev * tile_count
    kept_patches = patch_dev // band_count
    cosine_table, sine_table = fourier_tables(extent)
    col_upper, col_lower = fourier_pair(jnp.concatenate([cosine_table, -sine_table], axis=1))
    row_full = jnp.concatenate(
        [
            jnp.concatenate([cosine_table, sine_table], axis=1),
            jnp.concatenate([-sine_table, cosine_table], axis=1),
        ],
        axis=0,
    )
    row_upper, row_lower = fourier_pair(row_full)
    tile_at = lax.axis_index("tile")
    half_at = lax.axis_index("half")
    band_at = lax.axis_index("band")
    device_at = lax.axis_index(("tile", "half"))
    own_blocks = lax.dynamic_slice_in_dim(destination, device_at * group_size, group_size)
    send_order = jnp.argsort(own_blocks // group_size)
    inverse = (
        jnp.zeros_like(destination)
        .at[destination]
        .set(jnp.arange(destination.shape[0], dtype=jnp.int32))
    )
    opt_values = optical.astype(jnp.float32)
    opt_sums = jnp.sum(opt_values, axis=(2, 3))
    opt_squares = jnp.sum(opt_values * opt_values, axis=(2, 3))
    sar_values = sar.astype(jnp.float32).reshape(local_bands, group_size, block_lines * extent)
    sar_sums = jnp.sum(sar_values, axis=2)
    sar_squares = jnp.sum(sar_values * sar_values, axis=2)
    map_device = own_blocks // group_size
    map_patch = (
        map_device // half_count * patch_dev + own_blocks % group_size * block_lines // quarter
    )
    member = (map_patch[:, None] == jnp.arange(patch_total, dtype=jnp.int32)[None, :]).astype(
        jnp.float32
    )
    sar_stats = jnp.dot(
        jnp.stack([sar_sums, sar_squares]).reshape(2 * local_bands, group_size),
        member,
        precision=precise,
        preferred_element_type=jnp.float32,
    )
    statistics = jnp.zeros((2, 2, band_total, patch_total), jnp.float32)
    opt_part = jnp.transpose(jnp.stack([opt_sums, opt_squares]), (0, 2, 1))
    statistics = lax.dynamic_update_slice(
        statistics, opt_part[None], (0, 0, band_at * local_bands, tile_at * patch_dev)
    )
    statistics = lax.dynamic_update_slice(
        statistics,
        sar_stats.reshape(2, local_bands, patch_total)[None],
        (1, 0, band_at * local_bands, 0),
    )
    totals = lax.psum(statistics, ("tile", "half", "band"))
    centered = totals[:, 1] - totals[:, 0] * totals[:, 0] / pixel_count
    energy = jnp.sum(centered, axis=1) / (band_total * pixel_count)
    norm_scale = lax.rsqrt(band_total * pixel_count * (energy[0] + EPSILON) * (energy[1] + EPSILON))
    first_patch = tile_at * patch_dev + band_at * kept_patches
    norm_mine = lax.dynamic_slice_in_dim(norm_scale, first_patch, kept_patches)
    slant_spectra = column_spectrum(sar, col_upper, col_lower).reshape(
        local_bands, group_size, block_lines, 2, half_count, col_width
    )
    outgoing = jnp.take(slant_spectra, send_order, axis=1).reshape(
        local_bands, tile_count, half_count, block_lines, 2, half_count, col_width
    )
    outgoing = jnp.transpose(outgoing, (0, 1, 5, 2, 3, 4, 6))
    arrived = relay_blocks(outgoing).reshape(
        local_bands, group_size * half_count, block_lines, 2, col_width
    )
    sources = lax.dynamic_slice_in_dim(
        inverse, tile_at * half_count * group_size, half_count * group_size
    )
    slot_index = (
        sources // group_size * half_count
        + jnp.arange(half_count * group_size, dtype=jnp.int32) // group_size
    )
    placed = jnp.take(arrived, slot_index, axis=1).reshape(
        local_bands, half_count, patch_dev, quarter, 2, col_width
    )
    placed = jnp.transpose(placed, (2, 0, 1, 3, 4, 5)).reshape(
        patch_dev, local_bands, extent, 2, col_width
    )
    sar_real, sar_imag = row_spectrum(placed, row_upper, row_lower)
    spectra = column_spectrum(optical, col_upper, col_lower).reshape(
        patch_dev, local_bands, quarter, 2, half_count, col_width
    )
    real_part, imag_part = row_spectrum(
        jnp.squeeze(
            lax.all_to_all(spectra, "half", split_axis=4, concat_axis=2, tiled=True), axis=4
        ),
        row_upper,
        row_lower,
    )
    opt_real = real_part
    opt_imag = imag_part
    rows_at = jnp.arange(extent, dtype=jnp.int32)[:, None]
    cols_at = half_at * col_width + jnp.arange(col_width, dtype=jnp.int32)[None, :]
    keep_mask = jnp.where((rows_at == 0) & (cols_at == 0), 0.0, 1.0).astype(jnp.float32)
    opt_real = opt_real * keep_mask
    opt_imag = opt_imag * keep_mask
    sar_real = sar_real * keep_mask
    sar_imag = sar_imag * keep_mask
    cross_real = jnp.sum(opt_real * sar_real + opt_imag * sar_imag, axis=1)
    cross_imag = jnp.sum(opt_real * sar_imag - opt_imag * sar_real, axis=1)
    cross_term = jnp.stack([cross_real, cross_imag], axis=1)
    cross_sum = lax.psum_scatter(cross_term, "band", scatter_dimension=0, tiled=True)
    lag_real = (
        jnp.einsum("uk,pkc->puc", cosine_table, cross_sum[:, 0], precision=precise)
        - jnp.einsum("uk,pkc->puc", sine_table, cross_sum[:, 1], precision=precise)
    ) / extent
    lag_imag = (
        jnp.einsum("uk,pkc->puc", cosine_table, cross_sum[:, 1], precision=precise)
        + jnp.einsum("uk,pkc->puc", sine_table, cross_sum[:, 0], precision=precise)
    ) / extent
    lagged = jnp.stack([lag_real, lag_imag], axis=2).reshape(
        kept_patches, half_count, quarter, 2, col_width
    )
    pieces = lax.all_to_all(lagged, "half", split_axis=1, concat_axis=4, tiled=True)
    real_in = pieces[:, 0, :, 0, :]
    imag_in = pieces[:, 0, :, 1, :]
    correlation = (
        jnp.einsum("puc,cv->puv", real_in, cosine_table, precision=precise)
        - jnp.einsum("puc,cv->puv", imag_in, sine_table, precision=precise)
    ) / extent
    surface = correlation * norm_mine[:, None, None]
    local_rows = peaks[:, 0, :] - half_at * quarter
    row_hit = (
        local_rows[:, :, None] == jnp.arange(quarter, dtype=jnp.int32)[None, None, :]
    ).astype(jnp.float32)
    picked = jnp.einsum("pkr,prc->pkc", row_hit, surface, precision=precise)
    col_hit = (peaks[:, 1, :, None] == jnp.arange(extent, dtype=jnp.int32)[None, None, :]).astype(
        jnp.float32
    )
    local_values = jnp.sum(picked * col_hit, axis=2)
    peak_values = lax.psum(local_values, "half")
    return (surface, peak_values)


def half_tables(extent, half_count, chunk):
    width = extent // 2 // half_count
    places = np.arange(extent)
    phases = (places[:, None] * places[None, :]) % extent
    cosine = np.cos(phases * (2.0 * np.pi / extent))
    sine = np.sin(phases * (2.0 * np.pi / extent))
    forward, backward = [], []
    for half in range(half_count):
        span = slice(half * width, (half + 1) * width)
        real, imag = cosine[:, span].copy(), -sine[:, span]
        real_back, imag_back = 2.0 * cosine[span], -2.0 * sine[span]
        if half == 0:
            imag[:, 0] = cosine[:, extent // 2]
            real_back[0] = 1.0
            imag_back[0] = cosine[extent // 2]
        forward.append(np.concatenate([real, imag], axis=1))
        backward.append(np.concatenate([real_back, imag_back], axis=0))
    col_table = np.concatenate(forward, axis=1)
    lag_table = np.stack(backward)
    row_table = np.concatenate(
        [cosine.reshape(-1, chunk, extent), sine.reshape(-1, chunk, extent)], axis=1
    )
    return tuple(t.astype(jnp.bfloat16) for t in (col_table, row_table, lag_table))


def kernel(
    sizes,
    dest_hbm,
    peaks_hbm,
    sar_hbm,
    opt_hbm,
    col_hbm,
    row_hbm,
    lag_hbm,
    surface_ref,
    total_ref,
    dest_ref,
    peaks_ref,
    sar_v,
    opt_v,
    col_v,
    row_v,
    lag_v,
    sar_send,
    arrived,
    opt_send,
    opt_cols,
    sar_cols,
    sar_rows,
    cross_send,
    cross_recv,
    cross_own,
    cross_all,
    stat_send,
    stat_recv,
    last_send,
    last_recv,
    lags,
    lag_recv,
    load_sem,
    sar_ssem,
    sar_rsem,
    opt_ssem,
    opt_rsem,
    pair_ssem,
    pair_rsem,
):
    tiles, halves, bands, patch_dev, quarter, extent, lines, chunk, peak_count = sizes
    group = tiles * halves
    width = extent // 2 // halves
    chunks = extent // chunk
    per_half = chunks // halves
    tile, half, band = lax.axis_index("tile"), lax.axis_index("half"), lax.axis_index("band")
    me = tile * halves + half
    other_half = 1 - half
    other_band = 1 - band

    loads = [
        pltpu.make_async_copy(a, b, load_sem.at[i])
        for i, (a, b) in enumerate(
            [(sar_hbm, sar_v), (col_hbm, col_v), (opt_hbm, opt_v), (row_hbm, row_v), (lag_hbm, lag_v),
             (dest_hbm, dest_ref), (peaks_hbm, peaks_ref)]
        )
    ]
    for i in (5, 0, 1, 2):
        loads[i].start()

    barrier = pltpu.get_barrier_semaphore()
    for step in range(tiles):
        for shift in range(halves):
            if step or shift:
                pl.semaphore_signal(
                    barrier,
                    inc=1,
                    device_id={
                        "tile": lax.rem(tile + step, tiles),
                        "half": lax.rem(half + shift, halves),
                    },
                    device_id_type=MESH,
                )
    pl.semaphore_signal(barrier, inc=1, device_id={"band": other_band}, device_id_type=MESH)

    loads[5].wait()
    own_runs = [lax.div(dest_ref[me * group + j], group) for j in range(group)]

    def block_for(run):
        found = jnp.int32(0)
        for j in range(group):
            found = jnp.where(own_runs[j] == run, j, found)
        return found

    def sar_copy(step, shift):
        to_half = lax.rem(half + shift, halves)
        return pltpu.make_async_remote_copy(
            src_ref=sar_send.at[step, to_half],
            dst_ref=arrived.at[me],
            send_sem=sar_ssem.at[step * halves + shift],
            recv_sem=sar_rsem.at[me],
            device_id={"tile": lax.rem(tile + step, tiles), "half": to_half},
            device_id_type=MESH,
        )

    loads[0].wait()
    loads[1].wait()
    copies = []
    opt_copies = []
    order = sorted(range(tiles), key=lambda s: -min(s, tiles - s))
    for turn, step in enumerate(order):
        to_tile = lax.rem(tile + step, tiles)
        samples = jnp.concatenate(
            [sar_v[block_for(to_tile * halves + run)] for run in range(halves)], axis=0
        )
        spectra = jnp.dot(samples, col_v[...], preferred_element_type=jnp.float32)
        spectra = spectra.astype(jnp.bfloat16)
        for to_half in range(halves):
            piece = spectra[:, to_half * 2 * width : (to_half + 1) * 2 * width]
            sar_send[step, to_half] = piece.reshape(halves, lines, 2 * width)
        if turn == 0:
            for i in (3, 4, 6):
                loads[i].start()
        if turn == 1:
            pl.semaphore_wait(barrier, group)
        for ready in order[:2] if turn == 1 else (order[turn : turn + 1] if turn > 1 else ()):
            for shift in reversed(range(halves)):
                if ready or shift:
                    copy = sar_copy(ready, shift)
                    copy.start()
                    copies.append(copy)
    arrived[me] = sar_send[0, half]

    rows = pl.ds(pl.multiple_of(half * quarter, quarter), quarter)
    loads[2].wait()
    for turn, patch in enumerate((other_band, band)):
        spectra = jnp.dot(opt_v[patch], col_v[...], preferred_element_type=jnp.float32)
        spectra = spectra.astype(jnp.bfloat16)
        for to_half in range(halves):
            opt_send[turn, to_half] = spectra[:, to_half * 2 * width : (to_half + 1) * 2 * width]
        copy = pltpu.make_async_remote_copy(
            src_ref=opt_send.at[turn, other_half],
            dst_ref=opt_cols.at[turn, rows],
            send_sem=opt_ssem.at[turn],
            recv_sem=opt_rsem.at[turn],
            device_id={"half": other_half},
            device_id_type=MESH,
        )
        copy.start()
        opt_copies.append(copy)
        opt_cols[turn, rows, :] = opt_send[turn, half]

    slot_of = []
    for run in range(halves):
        places = []
        for source in range(group):
            place = jnp.int32(0)
            for j in range(group):
                spot = dest_ref[source * group + j]
                place = jnp.where(
                    lax.div(spot, group) == tile * halves + run, lax.rem(spot, group), place
                )
            places.append(place)
        for slot in range(group):
            found = jnp.int32(0)
            for source in range(group):
                found = jnp.where(places[source] == slot, source, found)
            slot_of.append(found)

    for step in order:
        for shift in range(halves):
            if step or shift:
                source = lax.rem(tile + step, tiles) * halves + lax.rem(half + shift, halves)
                pltpu.make_async_remote_copy(
                    src_ref=sar_send.at[0, 0],
                    dst_ref=arrived.at[source],
                    send_sem=sar_ssem.at[0],
                    recv_sem=sar_rsem.at[source],
                    device_id={"half": other_half},
                    device_id_type=MESH,
                ).wait_recv()
    per_patch = group // patch_dev
    for run in range(halves):
        for slot in range(group):
            at = run * quarter + (slot % per_patch) * lines
            sar_cols[slot // per_patch, at : at + lines, :] = arrived[slot_of[run * group + slot], run]

    loads[3].wait()
    for patch in range(patch_dev):
        for c in range(chunks):
            sar_rows[patch, c] = jnp.dot(
                row_v[c], sar_cols[patch], preferred_element_type=jnp.float32
            )

    lane = lax.broadcasted_iota(jnp.int32, (chunk, width), 1)
    line = lax.broadcasted_iota(jnp.int32, (chunk, width), 0)
    shared = (lane + half) == 0
    centre = (lane + line + half) == 0

    def parts(table_rows, first):
        a, c = table_rows[:chunk, :width], table_rows[:chunk, width:]
        b, d = table_rows[chunk:, :width], table_rows[chunk:, width:]
        if first:
            a = jnp.where(centre, 0.0, a)
        return a, b, c, d

    def cross_chunk(turn, patch, c):
        oa, ob, oc, od = parts(
            jnp.dot(row_v[c], opt_cols[turn], preferred_element_type=jnp.float32), c == 0
        )
        sa, sb, sc, sd = parts(sar_rows[patch, c], c == 0)
        o_re, o_im, s_re, s_im = oa + od, oc - ob, sa + sd, sc - sb
        real = o_re * s_re + o_im * s_im
        imag = o_re * s_im - o_im * s_re
        shared_real = oa * sa + ob * sb - (od * sc - oc * sd)
        shared_imag = ob * sa - oa * sb + (oc * sc + od * sd)
        real = jnp.where(shared, shared_real, real)
        imag = jnp.where(shared, shared_imag, imag)
        o_energy = jnp.sum(o_re * o_re + o_im * o_im, axis=0, keepdims=True)
        s_energy = jnp.sum(s_re * s_re + s_im * s_im, axis=0, keepdims=True)
        return real, imag, o_energy, s_energy

    weight = jnp.where(shared[:1], 1.0, 2.0)

    def pair_copy(k, src, dst, axis, to):
        return pltpu.make_async_remote_copy(
            src_ref=src,
            dst_ref=dst,
            send_sem=pair_ssem.at[k],
            recv_sem=pair_rsem.at[k],
            device_id={axis: to},
            device_id_type=MESH,
        )

    opt_copies[0].wait_recv()
    o_sum, s_sum = 0.0, 0.0
    for c in range(chunks):
        real, imag, o_energy, s_energy = cross_chunk(0, other_band, c)
        cross_send[c, :, :width] = real.astype(jnp.bfloat16)
        cross_send[c, :, width:] = imag.astype(jnp.bfloat16)
        o_sum, s_sum = o_sum + o_energy, s_sum + s_energy
    stat_send[0:1, :] = o_sum * weight
    stat_send[1:2, :] = s_sum * weight
    stat_send[2:8, :] = jnp.zeros((6, width), jnp.float32)
    cross_copy = pair_copy(0, cross_send, cross_recv, "band", other_band)
    cross_copy.start()
    stat_copy = pair_copy(1, stat_send, stat_recv, "band", other_band)
    stat_copy.start()

    opt_copies[1].wait_recv()
    o_sum, s_sum = 0.0, 0.0
    for c in range(chunks):
        real, imag, o_energy, s_energy = cross_chunk(1, band, c)
        cross_own[c, :, :width] = real
        cross_own[c, :, width:] = imag
        o_sum, s_sum = o_sum + o_energy, s_sum + s_energy

    cross_copy.wait_recv()
    for c in range(chunks):
        total = cross_own[c] + cross_recv[c].astype(jnp.float32)
        cross_all[c * chunk : (c + 1) * chunk, :] = total.astype(jnp.bfloat16)

    loads[4].wait()

    def lag_chunk(c):
        both = jnp.dot(row_v[c], cross_all[...], preferred_element_type=jnp.float32)
        lags[c, :, :width] = (both[:chunk, :width] - both[chunk:, width:]).astype(jnp.bfloat16)
        lags[c, :, width:] = (both[:chunk, width:] + both[chunk:, :width]).astype(jnp.bfloat16)

    lag_copies = []
    for i in range(per_half):
        at = other_half * per_half + i
        lag_chunk(at)
        copy = pair_copy(3 + i, lags.at[at], lag_recv.at[i], "half", other_half)
        copy.start()
        lag_copies.append(copy)
    for i in range(per_half):
        lag_chunk(half * per_half + i)

    spots = lax.broadcasted_iota(jnp.int32, (peak_count, extent), 1)
    ranks = lax.broadcasted_iota(jnp.int32, (peak_count, extent), 0)

    loads[6].wait()

    def one_hot(which):
        wanted = jnp.zeros((peak_count, extent), jnp.int32)
        for j in range(peak_count):
            wanted = jnp.where(ranks == j, peaks_ref[0, which, j], wanted)
        return jnp.where(spots == wanted, 1.0, 0.0).astype(jnp.bfloat16)

    picked = jnp.dot(
        one_hot(0), lags[...].reshape(extent, 2 * width), preferred_element_type=jnp.float32
    )
    waves = lax.dot_general(
        one_hot(1), lag_v[half], (((1,), (1,)), ((), ())), preferred_element_type=jnp.float32
    )
    stat_copy.wait_recv()
    last_send[0:8, :] = stat_recv[...]
    last_send[0:1, :] = o_sum * weight + stat_recv[0:1, :]
    last_send[1:2, :] = s_sum * weight + stat_recv[1:2, :]
    last_send[8 : 8 + peak_count, :] = jnp.broadcast_to(
        jnp.sum(picked * waves, axis=1, keepdims=True), (peak_count, width)
    )
    last_copy = pair_copy(2, last_send, last_recv, "half", other_half)
    last_copy.start()

    for i in range(per_half):
        at = slice(i * chunk, (i + 1) * chunk)
        near = lags[half * per_half + i]
        surface_ref[0, at, :] = jnp.dot(near, lag_v[half], preferred_element_type=jnp.float32)

    for i in range(per_half):
        at = slice(i * chunk, (i + 1) * chunk)
        lag_copies[i].wait_recv()
        far = jnp.dot(lag_recv[i], lag_v[other_half], preferred_element_type=jnp.float32)
        surface_ref[0, at, :] = surface_ref[0, at, :] + far

    last_copy.wait_recv()
    total_ref[...] = last_send[...] + last_recv[...]
    for copy in copies + opt_copies + lag_copies + [cross_copy, stat_copy, last_copy]:
        copy.wait_send()


def finish(bands, pieces, surface_ref, total_ref, out_ref, peak_ref, scaled, sem):
    _, lines, extent = surface_ref.shape
    pixels = extent * extent
    peak_count = peak_ref.shape[1]
    width = total_ref.shape[1]
    o_all = jnp.sum(total_ref[0:1, :], axis=1, keepdims=True) / (float(pixels) * bands * pixels)
    s_all = jnp.sum(total_ref[1:2, :], axis=1, keepdims=True) / (float(pixels) * bands * pixels)
    norm = lax.rsqrt(bands * pixels * (o_all + EPSILON) * (s_all + EPSILON)) / pixels
    part = lines // pieces
    copies = []
    for i in range(pieces):
        at = pl.ds(i * part, part)
        scaled[at, :] = surface_ref[0, at, :] * norm
        copy = pltpu.make_async_copy(scaled.at[at], out_ref.at[0, at], sem.at[i])
        copy.start()
        copies.append(copy)
    values = total_ref[8 : 8 + peak_count, :] * norm
    lane = lax.broadcasted_iota(jnp.int32, (peak_count, width), 1)
    rank = lax.broadcasted_iota(jnp.int32, (peak_count, width), 0)
    row = jnp.sum(jnp.where(lane == rank, values, 0.0), axis=0, keepdims=True)
    peak_ref[...] = row[:, :peak_count]
    for copy in copies:
        copy.wait()


def fused(mesh, optical, sar, destination, peaks):
    tiles, halves, bands = mesh.shape["tile"], mesh.shape["half"], mesh.shape["band"]
    patch_dev, _, quarter, extent = optical.shape
    group = tiles * halves
    lines = sar.shape[1] // group
    peak_count = peaks.shape[2]
    chunk = quarter // 2
    chunks = extent // chunk
    width = extent // 2 // halves
    sizes = (tiles, halves, bands, patch_dev, quarter, extent, lines, chunk, peak_count)
    tables = half_tables(extent, halves, chunk)
    bf, f32 = jnp.bfloat16, jnp.float32
    wide = 2 * width
    vmem = pltpu.VMEM
    dma = pltpu.SemaphoreType.DMA
    raw, totals = pl.pallas_call(
        functools.partial(kernel, sizes),
        out_shape=(
            jax.ShapeDtypeStruct((1, quarter, extent), f32),
            jax.ShapeDtypeStruct((8 + peak_count, width), f32),
        ),
        in_specs=[pl.BlockSpec(memory_space=pltpu.HBM)] * 7,
        out_specs=(pl.BlockSpec(memory_space=pltpu.VMEM), pl.BlockSpec(memory_space=pltpu.VMEM)),
        scratch_shapes=[
            pltpu.SMEM(destination.shape, jnp.int32),
            pltpu.SMEM(peaks.shape, jnp.int32),
            vmem((group, lines, extent), bf),
            vmem((patch_dev, quarter, extent), bf),
            vmem((extent, extent), bf),
            vmem((chunks, 2 * chunk, extent), bf),
            vmem((halves, wide, extent), bf),
            vmem((tiles, halves, halves, lines, wide), bf),
            vmem((group, halves, lines, wide), bf),
            vmem((patch_dev, halves, quarter, wide), bf),
            vmem((patch_dev, extent, wide), bf),
            vmem((patch_dev, extent, wide), bf),
            vmem((patch_dev, chunks, 2 * chunk, wide), f32),
            vmem((chunks, chunk, wide), bf),
            vmem((chunks, chunk, wide), bf),
            vmem((chunks, chunk, wide), f32),
            vmem((extent, wide), bf),
            vmem((8, width), f32),
            vmem((8, width), f32),
            vmem((8 + peak_count, width), f32),
            vmem((8 + peak_count, width), f32),
            vmem((chunks, chunk, wide), bf),
            vmem((chunks // halves, chunk, wide), bf),
            dma((7,)),
            dma((group,)),
            dma((group,)),
            dma((2,)),
            dma((2,)),
            dma((3 + chunks // halves,)),
            dma((3 + chunks // halves,)),
        ],
        compiler_params=pltpu.CompilerParams(
            collective_id=0, has_side_effects=True, vmem_limit_bytes=50 * 1024 * 1024
        ),
    )(
        *[
            pltpu.with_memory_space_constraint(x, pltpu.HBM)
            for x in (
                destination,
                peaks,
                sar.reshape(group, lines, extent),
                optical.reshape(patch_dev, quarter, extent),
                *[jnp.asarray(t) for t in tables],
            )
        ]
    )
    pieces = 4
    return pl.pallas_call(
        functools.partial(finish, bands, pieces),
        out_shape=(
            jax.ShapeDtypeStruct((1, quarter, extent), f32),
            jax.ShapeDtypeStruct((1, peak_count), f32),
        ),
        in_specs=[pl.BlockSpec(memory_space=pltpu.VMEM)] * 2,
        out_specs=(pl.BlockSpec(memory_space=pltpu.HBM), pl.BlockSpec(memory_space=pltpu.VMEM)),
        scratch_shapes=[vmem((quarter, extent), f32), dma((pieces,))],
    )(*[pltpu.with_memory_space_constraint(x, pltpu.VMEM) for x in (raw, totals)])


def fits(mesh, optical, sar, peaks):
    group = mesh.shape["tile"] * mesh.shape["half"]
    patch_dev, local_bands, quarter, extent = optical.shape
    lines = sar.shape[1] // group
    return (
        mesh.shape["half"] == 2
        and mesh.shape["band"] == 2
        and patch_dev == 2
        and local_bands == 1
        and lines % 16 == 0
        and quarter % lines == 0
        and extent % 512 == 0
        and peaks.shape[0] == 1
        and peaks.shape[2] % 8 == 0
    )


def solution(mesh):
    def local(optical, sar, destination, peaks):
        if fits(mesh, optical, sar, peaks):
            return fused(mesh, optical, sar, destination, peaks)
        return generic(optical, sar, destination, peaks)

    in_specs = (
        P(("scene", "tile"), "band", "half", None),
        P("band", ("scene", "tile", "half"), None),
        P("scene"),
        P(("scene", "tile", "band"), None, None),
    )
    out_specs = (P(("scene", "tile", "band"), "half", None), P(("scene", "tile", "band"), None))
    return jax.shard_map(local, mesh=mesh, in_specs=in_specs, out_specs=out_specs, check_vma=False)
```

profile of v0, /device:TPU:0, one launch (start us, length us, event | category | flops | bytes accessed | tf_op | source)
XLA Modules:
  0.0 26.8 jit_solution(5379853167961945702)
XLA Ops:
  0.6 24.7 %shard_map.86 = (f32[1,256,512]{2,1,0:T(8,128)S(1)}, f32[16,128]{1,0:T(8,128)S(1)}) custom-call(s32[64]{0:T(128)} %dest_hbm.1, s32[1,2,8]{2,1,0:T(2,128)} %peaks_hbm.1, bf16[8,64,512]{2,1,0:T(8,128)(2,1)} %bitcast.2, bf16[2,256,512]{2,1,0:T(8,128)(2,1)} %bitcast.3, bf16[512,512]{1,0:T(8,128)(2,1)} %constant.6.clone.col_hbm, ...), custom_call_target="tpu_custom_call" | custom-call | tf_op jit(solution)/shard_map/pallas_call | solution.py:584
  25.4 1.4 %shard_map.87 = (f32[1,256,512]{2,1,0:T(8,128)}, f32[1,8]{1,0:T(1,128)}) custom-call(f32[1,256,512]{2,1,0:T(8,128)S(1)} %get-tuple-element.4.surface_ref, f32[16,128]{1,0:T(8,128)S(1)} %get-tuple-element.5.total_ref), custom_call_target="tpu_custom_call" | custom-call | tf_op jit(solution)/shard_map/pallas_call | solution.py:640
where the time goes:
time: 26.9 us; the launch traced here: 26.8 us
  Pallas kernels  26.1 us (97%)
  between operations  0.64 us (2%)
    pallas_call x1, Pallas kernels, fused(): pl.pallas_call(functools.partial(kernel, sizes), out_shape=(jax.ShapeDtyp...  24.7 us
    pallas_call x1, Pallas kernels, fused(): pl.pallas_call(functools.partial(finish, bands, pieces), out_shape=(jax.S...  1.43 us

commit v1 on v0

v1 whole, which is shorter than its diff:
```python
import functools
import math

import jax
import jax.numpy as jnp
import numpy as np
from jax import lax
from jax.experimental import pallas as pl
from jax.experimental.pallas import tpu as pltpu
from jax.sharding import PartitionSpec as P

MESH = pl.DeviceIdType.MESH

precise = lax.Precision.HIGHEST
EPSILON = 1e-06


def fourier_tables(extent):
    places = jnp.arange(extent, dtype=jnp.int32)
    phases = places[:, None] * places[None, :] % extent
    angles = phases.astype(jnp.float32) * (2.0 * math.pi / extent)
    return (jnp.cos(angles), jnp.sin(angles))


def fourier_pair(table):
    upper = table.astype(jnp.bfloat16)
    lower = (table - upper.astype(jnp.float32)).astype(jnp.bfloat16)
    return (upper, lower)


def column_spectrum(samples, table_upper, table_lower):
    extent = samples.shape[-1]
    values = samples.reshape(-1, extent)
    spectrum = jnp.dot(values, table_upper, preferred_element_type=jnp.float32) + jnp.dot(
        values, table_lower, preferred_element_type=jnp.float32
    )
    return spectrum.astype(jnp.bfloat16).reshape(samples.shape[:-1] + (2 * extent,))


def row_spectrum(columns, table_upper, table_lower):
    line_count = columns.shape[-3]
    stacked = jnp.concatenate([columns[..., 0, :], columns[..., 1, :]], axis=-2)
    result = jnp.einsum("kr,...rc->...kc", table_upper, stacked, preferred_element_type=jnp.float32)
    result = result + jnp.einsum(
        "kr,...rc->...kc", table_lower, stacked, preferred_element_type=jnp.float32
    )
    return (result[..., :line_count, :], result[..., line_count:, :])


def relay_blocks(parcel):
    layout = parcel.shape
    merged = parcel.reshape(layout[:1] + (layout[1] * layout[2],) + layout[3:])
    arrived = lax.all_to_all(merged, ("tile", "half"), split_axis=1, concat_axis=1, tiled=True)
    return arrived.reshape(layout)


def generic(optical, sar, destination, peaks):
    tile_count = lax.axis_size("tile")
    half_count = lax.axis_size("half")
    band_count = lax.axis_size("band")
    group_size = tile_count * half_count
    patch_dev, local_bands, quarter, extent = optical.shape
    col_width = extent // half_count
    block_lines = sar.shape[1] // group_size
    band_total = local_bands * band_count
    pixel_count = extent * extent
    patch_total = patch_dev * tile_count
    kept_patches = patch_dev // band_count
    cosine_table, sine_table = fourier_tables(extent)
    col_upper, col_lower = fourier_pair(jnp.concatenate([cosine_table, -sine_table], axis=1))
    row_full = jnp.concatenate(
        [
            jnp.concatenate([cosine_table, sine_table], axis=1),
            jnp.concatenate([-sine_table, cosine_table], axis=1),
        ],
        axis=0,
    )
    row_upper, row_lower = fourier_pair(row_full)
    tile_at = lax.axis_index("tile")
    half_at = lax.axis_index("half")
    band_at = lax.axis_index("band")
    device_at = lax.axis_index(("tile", "half"))
    own_blocks = lax.dynamic_slice_in_dim(destination, device_at * group_size, group_size)
    send_order = jnp.argsort(own_blocks // group_size)
    inverse = (
        jnp.zeros_like(destination)
        .at[destination]
        .set(jnp.arange(destination.shape[0], dtype=jnp.int32))
    )
    opt_values = optical.astype(jnp.float32)
    opt_sums = jnp.sum(opt_values, axis=(2, 3))
    opt_squares = jnp.sum(opt_values * opt_values, axis=(2, 3))
    sar_values = sar.astype(jnp.float32).reshape(local_bands, group_size, block_lines * extent)
    sar_sums = jnp.sum(sar_values, axis=2)
    sar_squares = jnp.sum(sar_values * sar_values, axis=2)
    map_device = own_blocks // group_size
    map_patch = (
        map_device // half_count * patch_dev + own_blocks % group_size * block_lines // quarter
    )
    member = (map_patch[:, None] == jnp.arange(patch_total, dtype=jnp.int32)[None, :]).astype(
        jnp.float32
    )
    sar_stats = jnp.dot(
        jnp.stack([sar_sums, sar_squares]).reshape(2 * local_bands, group_size),
        member,
        precision=precise,
        preferred_element_type=jnp.float32,
    )
    statistics = jnp.zeros((2, 2, band_total, patch_total), jnp.float32)
    opt_part = jnp.transpose(jnp.stack([opt_sums, opt_squares]), (0, 2, 1))
    statistics = lax.dynamic_update_slice(
        statistics, opt_part[None], (0, 0, band_at * local_bands, tile_at * patch_dev)
    )
    statistics = lax.dynamic_update_slice(
        statistics,
        sar_stats.reshape(2, local_bands, patch_total)[None],
        (1, 0, band_at * local_bands, 0),
    )
    totals = lax.psum(statistics, ("tile", "half", "band"))
    centered = totals[:, 1] - totals[:, 0] * totals[:, 0] / pixel_count
    energy = jnp.sum(centered, axis=1) / (band_total * pixel_count)
    norm_scale = lax.rsqrt(band_total * pixel_count * (energy[0] + EPSILON) * (energy[1] + EPSILON))
    first_patch = tile_at * patch_dev + band_at * kept_patches
    norm_mine = lax.dynamic_slice_in_dim(norm_scale, first_patch, kept_patches)
    slant_spectra = column_spectrum(sar, col_upper, col_lower).reshape(
        local_bands, group_size, block_lines, 2, half_count, col_width
    )
    outgoing = jnp.take(slant_spectra, send_order, axis=1).reshape(
        local_bands, tile_count, half_count, block_lines, 2, half_count, col_width
    )
    outgoing = jnp.transpose(outgoing, (0, 1, 5, 2, 3, 4, 6))
    arrived = relay_blocks(outgoing).reshape(
        local_bands, group_size * half_count, block_lines, 2, col_width
    )
    sources = lax.dynamic_slice_in_dim(
        inverse, tile_at * half_count * group_size, half_count * group_size
    )
    slot_index = (
        sources // group_size * half_count
        + jnp.arange(half_count * group_size, dtype=jnp.int32) // group_size
    )
    placed = jnp.take(arrived, slot_index, axis=1).reshape(
        local_bands, half_count, patch_dev, quarter, 2, col_width
    )
    placed = jnp.transpose(placed, (2, 0, 1, 3, 4, 5)).reshape(
        patch_dev, local_bands, extent, 2, col_width
    )
    sar_real, sar_imag = row_spectrum(placed, row_upper, row_lower)
    spectra = column_spectrum(optical, col_upper, col_lower).reshape(
        patch_dev, local_bands, quarter, 2, half_count, col_width
    )
    real_part, imag_part = row_spectrum(
        jnp.squeeze(
            lax.all_to_all(spectra, "half", split_axis=4, concat_axis=2, tiled=True), axis=4
        ),
        row_upper,
        row_lower,
    )
    opt_real = real_part
    opt_imag = imag_part
    rows_at = jnp.arange(extent, dtype=jnp.int32)[:, None]
    cols_at = half_at * col_width + jnp.arange(col_width, dtype=jnp.int32)[None, :]
    keep_mask = jnp.where((rows_at == 0) & (cols_at == 0), 0.0, 1.0).astype(jnp.float32)
    opt_real = opt_real * keep_mask
    opt_imag = opt_imag * keep_mask
    sar_real = sar_real * keep_mask
    sar_imag = sar_imag * keep_mask
    cross_real = jnp.sum(opt_real * sar_real + opt_imag * sar_imag, axis=1)
    cross_imag = jnp.sum(opt_real * sar_imag - opt_imag * sar_real, axis=1)
    cross_term = jnp.stack([cross_real, cross_imag], axis=1)
    cross_sum = lax.psum_scatter(cross_term, "band", scatter_dimension=0, tiled=True)
    lag_real = (
        jnp.einsum("uk,pkc->puc", cosine_table, cross_sum[:, 0], precision=precise)
        - jnp.einsum("uk,pkc->puc", sine_table, cross_sum[:, 1], precision=precise)
    ) / extent
    lag_imag = (
        jnp.einsum("uk,pkc->puc", cosine_table, cross_sum[:, 1], precision=precise)
        + jnp.einsum("uk,pkc->puc", sine_table, cross_sum[:, 0], precision=precise)
    ) / extent
    lagged = jnp.stack([lag_real, lag_imag], axis=2).reshape(
        kept_patches, half_count, quarter, 2, col_width
    )
    pieces = lax.all_to_all(lagged, "half", split_axis=1, concat_axis=4, tiled=True)
    real_in = pieces[:, 0, :, 0, :]
    imag_in = pieces[:, 0, :, 1, :]
    correlation = (
        jnp.einsum("puc,cv->puv", real_in, cosine_table, precision=precise)
        - jnp.einsum("puc,cv->puv", imag_in, sine_table, precision=precise)
    ) / extent
    surface = correlation * norm_mine[:, None, None]
    local_rows = peaks[:, 0, :] - half_at * quarter
    row_hit = (
        local_rows[:, :, None] == jnp.arange(quarter, dtype=jnp.int32)[None, None, :]
    ).astype(jnp.float32)
    picked = jnp.einsum("pkr,prc->pkc", row_hit, surface, precision=precise)
    col_hit = (peaks[:, 1, :, None] == jnp.arange(extent, dtype=jnp.int32)[None, None, :]).astype(
        jnp.float32
    )
    local_values = jnp.sum(picked * col_hit, axis=2)
    peak_values = lax.psum(local_values, "half")
    return (surface, peak_values)


def dft_tables(extent, parts):
    points = extent // 2
    cols = points // parts // 2
    places = np.arange(extent)
    phases = (places[:, None] * places[None, :]) % extent
    cosine = np.cos(phases * (2.0 * np.pi / extent))
    sine = np.sin(phases * (2.0 * np.pi / extent))
    forward, backward = [], [[], []]
    for part in range(parts):
        for turn in range(2):
            first = (2 * part + turn) * cols
            span = slice(first, first + cols)
            real, imag = cosine[:, span].copy(), -sine[:, span]
            real_back, imag_back = 2.0 * cosine[span], -2.0 * sine[span]
            if first == 0:
                imag[:, 0] = cosine[:, points]
                real_back[0] = 1.0
                imag_back[0] = cosine[points]
            forward += [real, imag]
            backward[turn] += [real_back, imag_back]
    col_table = np.concatenate(forward, axis=1)
    back_table = np.stack([np.concatenate(b, axis=0) for b in backward])
    row_sine = sine[:points, :points].copy()
    row_sine[0] = cosine[points, :points]
    row_table = np.concatenate([cosine[:points, :points], row_sine], axis=0)
    lag_cosine, lag_sine = 2.0 * cosine[:, :points], 2.0 * sine[:, :points]
    lag_cosine[:, 0] = 1.0
    lag_sine[:, 0] = cosine[:, points]
    lag_table = np.concatenate([lag_cosine, lag_sine], axis=1)
    return tuple(t.astype(jnp.bfloat16) for t in (col_table, row_table, lag_table, back_table))


def kernel(
    sizes,
    dest_hbm,
    peaks_hbm,
    sar_hbm,
    opt_hbm,
    col_hbm,
    row_hbm,
    lag_hbm,
    back_hbm,
    surface_ref,
    total_ref,
    dest_ref,
    peaks_ref,
    sar_v,
    opt_v,
    col_v,
    row_v,
    lag_v,
    back_v,
    send_0,
    send_1,
    arrived_0,
    arrived_1,
    opt_send,
    opt_in,
    opt_waves,
    sar_cols,
    sar_rows,
    cross,
    lags,
    lag_send,
    lag_in,
    spot_send,
    spot_recv,
    last_mine,
    last_other,
    last_in,
    load_sem,
    sar_ssem,
    sar_rsem,
    opt_ssem,
    opt_rsem,
    lag_ssem,
    lag_rsem,
    last_ssem,
    last_rsem,
    spot_ssem,
    spot_rsem,
    near_sem,
    far_sem,
):
    tiles, halves, bands, patch_dev, quarter, extent, lines, peak_count = sizes
    group = tiles * halves
    parts = halves * bands
    wide = extent // parts
    side = wide // 2
    cols = wide // 4
    points = extent // 2
    per_patch = group // patch_dev
    send, arrived = (send_0, send_1), (arrived_0, arrived_1)
    f32, bf = jnp.float32, jnp.bfloat16
    tile, half, band = lax.axis_index("tile"), lax.axis_index("half"), lax.axis_index("band")
    me = tile * halves + half
    part = half * bands + band
    other_half = 1 - half
    other_band = 1 - band

    def place(step, shift, swap):
        return (
            lax.rem(tile + step, tiles),
            lax.rem(half + shift, halves),
            lax.rem(band + swap, bands),
        )

    def device(step, shift, swap):
        return dict(zip(("tile", "half", "band"), place(step, shift, swap)))

    others = tiles * parts - 1
    near = [(0, shift, swap) for shift in (1, 0) for swap in range(bands) if shift or swap]

    loads = [
        pltpu.make_async_copy(a, b, load_sem.at[i])
        for i, (a, b) in enumerate(
            [(dest_hbm, dest_ref), (sar_hbm, sar_v), (col_hbm, col_v), (opt_hbm, opt_v),
             (row_hbm, row_v), (peaks_hbm, peaks_ref), (lag_hbm, lag_v), (back_hbm, back_v)]
        )
    ]
    for i in (3, 2, 0, 1):
        loads[i].start()

    barrier = pltpu.get_barrier_semaphore()
    first_band, last_band = jnp.int32(0), jnp.int32(bands - 1)

    def tell(semaphore, **where):
        pl.semaphore_signal(semaphore, inc=1, device_id=where, device_id_type=MESH)

    for shift in range(1, halves):
        tell(barrier, half=lax.rem(half + shift, halves), band=first_band)
    pl.when(band != first_band)(lambda: tell(barrier, band=first_band))
    for step in sorted(range(1, tiles), key=lambda s: -min(s, tiles - s)):
        for shift in range(halves):
            tell(
                barrier,
                tile=lax.rem(tile + step, tiles),
                half=lax.rem(half + shift, halves),
                band=last_band,
            )

    def remote(src, dst, ssem, rsem, peer):
        return pltpu.make_async_remote_copy(
            src_ref=src,
            dst_ref=dst,
            send_sem=ssem,
            recv_sem=rsem,
            device_id=device(*peer),
            device_id_type=MESH,
        )

    source_at = me * bands + band

    def sar_copy(turn, to_tile, to_half, to_band):
        return pltpu.make_async_remote_copy(
            src_ref=send[turn].at[to_tile * parts + to_half * bands + to_band],
            dst_ref=arrived[turn].at[source_at],
            send_sem=sar_ssem.at[turn],
            recv_sem=sar_rsem.at[turn],
            device_id={"tile": to_tile, "half": to_half, "band": to_band},
            device_id_type=MESH,
        )

    low = lax.broadcasted_iota(jnp.int32, (1, wide), 1) < side

    def pair(a, b):
        first = jnp.concatenate([a[:, :side], b[:, :side]], axis=1)
        second = jnp.concatenate([a[:, side:], b[:, side:]], axis=1)
        return first, second

    def whole(ref, count, ssem, rsem):
        ref = ref.at[pl.ds(0, count)]
        return remote(ref, ref, ssem, rsem, (0, 1, 0))

    loads[0].wait()
    own_runs = [lax.div(dest_ref[me * group + j], group) for j in range(group)]

    def block_for(run):
        found = jnp.int32(0)
        for j in range(group):
            found = jnp.where(own_runs[j] == run, j, found)
        return found

    def sar_columns(to_tile):
        if to_tile == 0:
            loads[1].wait()
        samples = jnp.concatenate(
            [sar_v[block_for(to_tile * halves + run)] for run in range(halves)], axis=0
        )
        spectra = jnp.dot(samples, col_v[...], preferred_element_type=f32).astype(bf)
        for to in range(parts):
            at = slice(to * wide, (to + 1) * wide)
            first, second = pair(spectra[:lines, at], spectra[lines:, at])
            send_0[to_tile * parts + to] = first
            send_1[to_tile * parts + to] = second

    def sar_sends(turn, to_tile, shifts):
        for shift in shifts:
            to_half = lax.rem(half + shift, halves)
            for swap in range(bands):
                to_band = lax.rem(band + swap, bands)
                copy = sar_copy(turn, to_tile, to_half, to_band)
                if shift or swap:
                    copy.start()
                else:
                    pl.when(tile != to_tile)(copy.start)

    def opt_copy(turn, peer):
        _, to_half, to_band = place(*peer)
        return remote(
            opt_send.at[turn, to_half * bands + to_band],
            opt_in.at[turn, part],
            opt_ssem.at[turn],
            opt_rsem.at[turn],
            peer,
        )

    def opt_sends(turn):
        for peer in near:
            opt_copy(turn, peer).start()

    loads[3].wait()
    loads[2].wait()
    opt_spectra = [
        jnp.dot(opt_v[patch], col_v[...], preferred_element_type=f32).astype(bf)
        for patch in range(patch_dev)
    ]
    for to in range(parts):
        at = slice(to * wide, (to + 1) * wide)
        first, second = pair(*[s[:, at] for s in opt_spectra])
        opt_send[0, to] = first
        opt_send[1, to] = second
    @pl.when(band == first_band)
    def _():
        pl.semaphore_wait(barrier, parts - 1)
        tell(near_sem, band=last_band)

    @pl.when(band == last_band)
    def _():
        pl.semaphore_wait(near_sem, 1)

    opt_sends(0)
    opt_sends(1)
    sar_columns(0)
    for i in (4, 5, 6, 7):
        loads[i].start()

    @pl.when(band == last_band)
    def _():
        pl.semaphore_wait(barrier, (tiles - 1) * parts)
        tell(far_sem, band=first_band)

    @pl.when(band == first_band)
    def _():
        pl.semaphore_wait(far_sem, 1)

    sar_sends(0, 0, (0, 1))
    for to_tile in range(1, tiles):
        sar_columns(to_tile)
        sar_sends(0, to_tile, (0, 1))
    for to_tile in range(tiles):
        sar_sends(1, to_tile, (0,))
    arrived_0[source_at] = send_0[tile * parts + part]
    arrived_1[source_at] = send_1[tile * parts + part]
    for turn in range(2):
        opt_in[turn, part] = opt_send[turn, part]

    slot_of = []
    for run in range(halves):
        places = []
        for source in range(group):
            found = jnp.int32(0)
            for j in range(group):
                spot = dest_ref[source * group + j]
                found = jnp.where(
                    lax.div(spot, group) == tile * halves + run, lax.rem(spot, group), found
                )
            places.append(found)
        for slot in range(group):
            found = jnp.int32(0)
            for source in range(group):
                found = jnp.where(places[source] == slot, source, found)
            slot_of.append(found)

    spots = lax.broadcasted_iota(jnp.int32, (peak_count, extent), 1)
    ranks = lax.broadcasted_iota(jnp.int32, (peak_count, extent), 0)
    loads[5].wait()
    for which in range(2):
        wanted = jnp.zeros((peak_count, extent), jnp.int32)
        for j in range(peak_count):
            wanted = jnp.where(ranks == j, peaks_ref[0, which, j], wanted)
        spot_send[which * peak_count : (which + 1) * peak_count, :] = jnp.where(
            spots == wanted, 1.0, 0.0
        ).astype(bf)
    spot_copy = remote(spot_send, spot_recv, spot_ssem, spot_rsem, (0, 0, 1))
    spot_copy.start()

    lane = lax.broadcasted_iota(jnp.int32, (1, wide), 1)
    inner = lax.rem(lane, side)
    real_lane = inner < cols
    row_at = lax.broadcasted_iota(jnp.int32, (points, 1), 0)
    sign = jnp.where(lax.rem(row_at, 2) == 0, 1.0, -1.0)
    edge_real = [((inner + part + turn) == 0) for turn in range(2)]
    edge_imag = [((jnp.abs(inner - cols) + part + turn) == 0) for turn in range(2)]
    weights = [
        jnp.where(edge_real[turn] | edge_imag[turn], 1.0, 2.0) * float(extent)
        for turn in range(2)
    ]

    def turned(z, turn):
        ahead = pltpu.roll(z, wide - cols, 1)
        behind = pltpu.roll(z, cols, 1)
        return jnp.where(real_lane, -ahead, behind)

    opt_energy = [0.0, 0.0]

    def optical(turn):
        whole(opt_in.at[turn], parts - 1, opt_ssem.at[turn], opt_rsem.at[turn]).wait_recv()
        if turn == 0:
            for to_tile in range(tiles):
                sar_sends(1, to_tile, (1,))
        for source in range(bands):
            both = jnp.concatenate(
                [opt_in[turn, run * bands + source] for run in range(halves)], axis=1
            )
            rows = jnp.dot(row_v[...], both, preferred_element_type=f32)
            mean = jnp.where(
                edge_real[turn], (rows[0:1, :wide] + rows[0:1, wide:]) / float(extent), 0.0
            )
            total = 0.0
            for run in range(halves):
                moved = both[:, run * wide : (run + 1) * wide].astype(f32) - mean
                total = total + jnp.sum(moved * moved, axis=0, keepdims=True)
            opt_energy[turn] = opt_energy[turn] + total * weights[turn]
            for kind in range(2):
                at = slice(kind * points, (kind + 1) * points)
                near_rows, far_rows = rows[at, :wide], rows[at, wide:] * sign
                z = near_rows + far_rows
                z_far = pltpu.roll(z, side, 1)
                signed, signed_far = z * sign, z_far * sign
                for patch in range(patch_dev):
                    if patch == 0:
                        own = jnp.where(low, z, signed_far)
                    else:
                        own = jnp.where(low, z_far, signed)
                    other = jnp.where(
                        edge_real[turn], 0.0, jnp.where(edge_imag[turn], own, turned(own, turn))
                    )
                    own = jnp.where(edge_imag[turn], 0.0, own)
                    if kind == 0:
                        own = jnp.where(edge_real[turn] & (row_at == 0), 0.0, own)
                    opt_waves[turn, patch, source, kind] = own
                    opt_waves[turn, patch, source, 2 + kind] = other

    block = points // 4
    top = lax.broadcasted_iota(jnp.int32, (block, 1), 0) == 0

    def fold(a, b, c, d):
        def halve(u, v):
            return jnp.where(low, u, v) + pltpu.roll(jnp.where(low, v, u), side, 1)

        u, v = halve(a, c), halve(b, d)
        rest = jnp.where(real_lane, v, u)
        rest = jnp.where(
            real_lane, pltpu.roll(rest, wide - cols, 1), pltpu.roll(rest, cols, 1)
        )
        return jnp.where(real_lane, u, v) + rest

    def slant(turn):
        whole(arrived[turn], others, sar_ssem.at[turn], sar_rsem.at[turn]).wait_recv()
        if turn:
            for shift in (1, 0):
                lag_sends(0, shift)
        for slot in range(group):
            patch, at = slot // per_patch, slot % per_patch * lines
            for source in range(bands):
                pieces = [
                    arrived[turn][slot_of[run * group + slot] * bands + source]
                    for run in range(halves)
                ]
                sar_cols[turn, patch, at : at + lines, source * wide : (source + 1) * wide] = (
                    jnp.concatenate([pieces[0][:, :side], pieces[1][:, side:]], axis=1)
                )
        for patch in range(patch_dev):
            sar_rows[turn, patch] = jnp.dot(
                row_v[...], sar_cols[turn, patch], preferred_element_type=f32
            )
        for b in range(points // block):
            at = slice(b * block, (b + 1) * block)
            lower = slice(points + b * block, points + (b + 1) * block)
            sums = [[], [], [], []]
            for patch in range(patch_dev):
                e_re, e_im, d_lo, d_hi = 0.0, 0.0, 0.0, 0.0
                for source in range(bands):
                    lanes = slice(source * wide, (source + 1) * wide)
                    yc, ys = sar_rows[turn, patch, at, lanes], sar_rows[turn, patch, lower, lanes]
                    zc, zs, tc, ts = [opt_waves[turn, patch, source, k, at] for k in range(4)]
                    if b == 0:
                        zs_e = jnp.where(top, 0.0, zs)
                        ts_e = jnp.where(top, 0.0, ts)
                        zc_d = jnp.where(top, zs, zc)
                        tc_d = jnp.where(top, ts, tc)
                    else:
                        zs_e, ts_e, zc_d, tc_d = zs, ts, zc, tc
                    e_re = e_re + (zc * yc + zs_e * ys)
                    e_im = e_im + (tc * yc + ts_e * ys)
                    d_lo = d_lo + (zc_d * ys - zs_e * yc)
                    d_hi = d_hi + (tc_d * ys - ts_e * yc)
                for k, term in enumerate((e_re, e_im, d_lo, d_hi)):
                    sums[k].append(term)
            cross[turn, at, :] = fold(sums[0][0], sums[1][0], sums[0][1], sums[1][1]).astype(bf)
            cross[turn, lower, :] = fold(sums[2][0], sums[3][0], sums[2][1], sums[3][1]).astype(bf)

    def lag_copy(turn, peer):
        _, to_half, to_band = place(*peer)
        return remote(
            lag_send.at[turn, to_half * bands + to_band],
            lag_in.at[turn, part],
            lag_ssem.at[turn],
            lag_rsem.at[turn, peer[1]],
            peer,
        )

    def lag_sends(turn, shift):
        for swap in range(bands):
            if shift or swap:
                lag_copy(turn, (0, shift, swap)).start()

    def spread(turn):
        for shift, to_half in ((1, other_half), (0, half)):
            at = pl.ds(pl.multiple_of(to_half * quarter, quarter), quarter)
            values = jnp.dot(lag_v[at, :], cross[turn], preferred_element_type=f32).astype(bf)
            lags[turn, at, :] = values
            for patch, piece in enumerate(pair(values[: quarter // 2], values[quarter // 2 :])):
                lag_send[turn, to_half * bands + patch] = piece
            if turn:
                lag_sends(turn, shift)
        lag_in[turn, part] = lag_send[turn, part]

    def gather(turn, shift, first):
        from_half = lax.rem(half + shift, halves)
        count = bands if shift else bands - 1
        whole(lag_in.at[turn], count, lag_ssem.at[turn], lag_rsem.at[turn, shift]).wait_recv()
        upper, lower = pair(*[lag_in[turn, from_half * bands + b] for b in range(bands)])
        table = back_v[turn, pl.ds(pl.multiple_of(from_half * wide, wide), wide), :]
        values = jnp.dot(
            jnp.concatenate([upper, lower], axis=0), table, preferred_element_type=f32
        )
        if first:
            surface_ref[0] = values
        else:
            surface_ref[0] = surface_ref[0] + values

    loads[4].wait()
    optical(0)
    slant(0)
    loads[6].wait()
    spread(0)
    loads[7].wait()
    optical(1)
    slant(1)
    spread(1)

    sar_energy = []
    for patch in range(patch_dev):
        energy = 0.0
        for turn in range(2):
            for source in range(bands):
                lanes = slice(source * wide, (source + 1) * wide)
                head = sar_rows[turn, patch, 0:1, lanes]
                head = (head + pltpu.roll(head, side, 1)) / float(extent)
                mean = jnp.where(edge_real[turn], head, 0.0)
                moved = sar_cols[turn, patch, :, lanes].astype(f32) - mean
                energy = energy + jnp.sum(moved * moved, axis=0, keepdims=True) * weights[turn]
        sar_energy.append(energy)
    opt_total = opt_energy[0] + opt_energy[1]

    spot_copy.wait_recv()
    hits = jnp.concatenate([spot_send[...], spot_recv[...]], axis=0)
    found = 0.0
    for turn in range(2):
        picked = jnp.dot(hits, lags[turn], preferred_element_type=f32)
        rows_back = back_v[turn, pl.ds(pl.multiple_of(part * side, side), side), :]
        waves = lax.dot_general(
            hits,
            jnp.concatenate([rows_back, rows_back], axis=0),
            (((1,), (1,)), ((), ())),
            preferred_element_type=f32,
        )
        found = found + jnp.concatenate(
            [
                picked[:peak_count] * waves[peak_count : 2 * peak_count],
                picked[2 * peak_count : 3 * peak_count] * waves[3 * peak_count :],
            ],
            axis=0,
        )
    for which, patch, ref in ((0, band, last_mine), (1, other_band, last_other)):
        mine = lax.div(lane, side) == patch
        ref[0:8, :] = jnp.zeros((8, wide), f32)
        ref[0:1, :] = jnp.where(mine, opt_total, 0.0)
        ref[1:2, :] = jnp.where(patch == 0, sar_energy[0], sar_energy[1])
        value = jnp.where(mine, found[which * peak_count : (which + 1) * peak_count], 0.0)
        ref[8 : 8 + peak_count, :] = jnp.broadcast_to(
            jnp.sum(value, axis=1, keepdims=True), (peak_count, wide)
        )
    for peer in near:
        remote(
            last_other if peer[2] else last_mine, last_in.at[part], last_ssem, last_rsem, peer
        ).start()

    gather(0, 0, True)
    gather(1, 0, False)
    gather(0, 1, False)
    gather(1, 1, False)
    whole(last_in, parts - 1, last_ssem, last_rsem).wait_recv()
    last_in[part] = last_mine[...]
    total_ref[...] = sum(last_in[i] for i in range(1, parts)) + last_in[0]
    for turn in range(2):
        whole(send[turn], others, sar_ssem.at[turn], sar_rsem.at[turn]).wait_send()
        whole(opt_in.at[turn], parts - 1, opt_ssem.at[turn], opt_rsem.at[turn]).wait_send()
        whole(lag_in.at[turn], parts - 1, lag_ssem.at[turn], lag_rsem.at[turn, 0]).wait_send()
    whole(last_in, parts - 1, last_ssem, last_rsem).wait_send()
    spot_copy.wait_send()


def finish(bands, pieces, surface_ref, total_ref, out_ref, peak_ref, scaled, sem):
    _, lines, extent = surface_ref.shape
    pixels = extent * extent
    peak_count = peak_ref.shape[1]
    width = total_ref.shape[1]
    o_all = jnp.sum(total_ref[0:1, :], axis=1, keepdims=True) / (float(pixels) * bands * pixels)
    s_all = jnp.sum(total_ref[1:2, :], axis=1, keepdims=True) / (float(pixels) * bands * pixels)
    norm = lax.rsqrt(bands * pixels * (o_all + EPSILON) * (s_all + EPSILON)) / pixels
    part = lines // pieces
    copies = []
    for i in range(pieces):
        at = pl.ds(i * part, part)
        scaled[at, :] = surface_ref[0, at, :] * norm
        copy = pltpu.make_async_copy(scaled.at[at], out_ref.at[0, at], sem.at[i])
        copy.start()
        copies.append(copy)
    values = total_ref[8 : 8 + peak_count, :] * norm
    lane = lax.broadcasted_iota(jnp.int32, (peak_count, width), 1)
    rank = lax.broadcasted_iota(jnp.int32, (peak_count, width), 0)
    row = jnp.sum(jnp.where(lane == rank, values, 0.0), axis=0, keepdims=True)
    peak_ref[...] = row[:, :peak_count]
    for copy in copies:
        copy.wait()


def fused(mesh, optical, sar, destination, peaks):
    tiles, halves, bands = mesh.shape["tile"], mesh.shape["half"], mesh.shape["band"]
    patch_dev, _, quarter, extent = optical.shape
    group = tiles * halves
    parts = halves * bands
    lines = sar.shape[1] // group
    peak_count = peaks.shape[2]
    wide = extent // parts
    points = extent // 2
    sizes = (tiles, halves, bands, patch_dev, quarter, extent, lines, peak_count)
    tables = dft_tables(extent, parts)
    bf, f32 = jnp.bfloat16, jnp.float32
    vmem = pltpu.VMEM
    dma = pltpu.SemaphoreType.DMA
    raw, totals = pl.pallas_call(
        functools.partial(kernel, sizes),
        out_shape=(
            jax.ShapeDtypeStruct((1, quarter, extent), f32),
            jax.ShapeDtypeStruct((8 + peak_count, wide), f32),
        ),
        in_specs=[pl.BlockSpec(memory_space=pltpu.HBM)] * 8,
        out_specs=(pl.BlockSpec(memory_space=pltpu.VMEM), pl.BlockSpec(memory_space=pltpu.VMEM)),
        scratch_shapes=[
            pltpu.SMEM(destination.shape, jnp.int32),
            pltpu.SMEM(peaks.shape, jnp.int32),
            vmem((group, lines, extent), bf),
            vmem((patch_dev, quarter, extent), bf),
            vmem((extent, extent), bf),
            vmem((extent, points), bf),
            vmem((extent, extent), bf),
            vmem((2, points, extent), bf),
            vmem((tiles * parts, lines, wide), bf),
            vmem((tiles * parts, lines, wide), bf),
            vmem((group * bands, lines, wide), bf),
            vmem((group * bands, lines, wide), bf),
            vmem((2, parts, quarter, wide), bf),
            vmem((2, parts, quarter, wide), bf),
            vmem((2, patch_dev, bands, 4, points, wide), f32),
            vmem((2, patch_dev, points, bands * wide), bf),
            vmem((2, patch_dev, extent, bands * wide), f32),
            vmem((2, extent, wide), bf),
            vmem((2, extent, wide), bf),
            vmem((2, parts, quarter // 2, wide), bf),
            vmem((2, parts, quarter // 2, wide), bf),
            vmem((2 * peak_count, extent), bf),
            vmem((2 * peak_count, extent), bf),
            vmem((8 + peak_count, wide), f32),
            vmem((8 + peak_count, wide), f32),
            vmem((parts, 8 + peak_count, wide), f32),
            dma((8,)),
            dma((2,)),
            dma((2,)),
            dma((2,)),
            dma((2,)),
            dma((2,)),
            dma((2, 2)),
            dma,
            dma,
            dma,
            dma,
            pltpu.SemaphoreType.REGULAR,
            pltpu.SemaphoreType.REGULAR,
        ],
        compiler_params=pltpu.CompilerParams(
            collective_id=0, has_side_effects=True, vmem_limit_bytes=50 * 1024 * 1024
        ),
    )(
        *[
            pltpu.with_memory_space_constraint(x, pltpu.HBM)
            for x in (
                destination,
                peaks,
                sar.reshape(group, lines, extent),
                optical.reshape(patch_dev, quarter, extent),
                *[jnp.asarray(t) for t in tables],
            )
        ]
    )
    pieces = 4
    return pl.pallas_call(
        functools.partial(finish, bands, pieces),
        out_shape=(
            jax.ShapeDtypeStruct((1, quarter, extent), f32),
            jax.ShapeDtypeStruct((1, peak_count), f32),
        ),
        in_specs=[pl.BlockSpec(memory_space=pltpu.VMEM)] * 2,
        out_specs=(pl.BlockSpec(memory_space=pltpu.HBM), pl.BlockSpec(memory_space=pltpu.VMEM)),
        scratch_shapes=[vmem((quarter, extent), f32), dma((pieces,))],
    )(*[pltpu.with_memory_space_constraint(x, pltpu.VMEM) for x in (raw, totals)])


def fits(mesh, optical, sar, peaks):
    group = mesh.shape["tile"] * mesh.shape["half"]
    patch_dev, local_bands, quarter, extent = optical.shape
    lines = sar.shape[1] // group
    return (
        mesh.shape["half"] == 2
        and mesh.shape["band"] == 2
        and patch_dev == 2
        and local_bands == 1
        and lines % 16 == 0
        and quarter * 2 == extent
        and group * lines == patch_dev * quarter
        and extent % 512 == 0
        and peaks.shape[0] == 1
        and peaks.shape[2] % 8 == 0
    )


def solution(mesh):
    def local(optical, sar, destination, peaks):
        if fits(mesh, optical, sar, peaks):
            return fused(mesh, optical, sar, destination, peaks)
        return generic(optical, sar, destination, peaks)

    in_specs = (
        P(("scene", "tile"), "band", "half", None),
        P("band", ("scene", "tile", "half"), None),
        P("scene"),
        P(("scene", "tile", "band"), None, None),
    )
    out_specs = (P(("scene", "tile", "band"), "half", None), P(("scene", "tile", "band"), None))
    return jax.shard_map(local, mesh=mesh, in_specs=in_specs, out_specs=out_specs, check_vma=False)
```

time: 26.9 us -> 26.3 us (0.978)
  Pallas kernels: 26.1 us -> 25.6 us
    pallas_call x1, Pallas kernels: 24.7 us -> 24.1 us  [fused(): pl.pallas_call(functools.partial(kernel, sizes), out_shape=(jax.ShapeDtyp...]
where the time goes in v1:
time: 26.3 us; the launch traced here: 26.2 us
  Pallas kernels  25.6 us (97%)
  between operations  0.64 us (2%)
    pallas_call x1, Pallas kernels, fused(): pl.pallas_call(functools.partial(kernel, sizes), out_shape=(jax.ShapeDtyp...  24.1 us
    pallas_call x1, Pallas kernels, fused(): pl.pallas_call(functools.partial(finish, bands, pieces), out_shape=(jax.S...  1.43 us

profile of v1, /device:TPU:0, one launch (start us, length us, event | category | flops | bytes accessed | tf_op | source)
XLA Modules:
  0.0 26.2 jit_solution(1512227764025577771)
XLA Ops:
  0.6 24.1 %shard_map.95 = (f32[1,256,512]{2,1,0:T(8,128)S(1)}, f32[16,128]{1,0:T(8,128)S(1)}) custom-call(s32[64]{0:T(128)} %dest_hbm.1, s32[1,2,8]{2,1,0:T(2,128)} %peaks_hbm.1, bf16[8,64,512]{2,1,0:T(8,128)(2,1)} %bitcast.2, bf16[2,256,512]{2,1,0:T(8,128)(2,1)} %bitcast.3, bf16[512,512]{1,0:T(8,128)(2,1)} %constant.8.clone.col_hbm, ...), custom_call_target="tpu_custom_call" | custom-call | tf_op jit(solution)/shard_map/pallas_call | solution.py:768
  24.8 1.4 %shard_map.96 = (f32[1,256,512]{2,1,0:T(8,128)}, f32[1,8]{1,0:T(1,128)}) custom-call(f32[1,256,512]{2,1,0:T(8,128)S(1)} %get-tuple-element.4.surface_ref, f32[16,128]{1,0:T(8,128)S(1)} %get-tuple-element.5.total_ref), custom_call_target="tpu_custom_call" | custom-call | tf_op jit(solution)/shard_map/pallas_call | solution.py:833

commit v2 on v1

--- a/solution.py
+++ b/solution.py
@@ -13,6 +13,7 @@
 
 precise = lax.Precision.HIGHEST
 EPSILON = 1e-06
+BLOCK = 16
 
 
 def fourier_tables(extent):
@@ -223,13 +224,19 @@
             backward[turn] += [real_back, imag_back]
     col_table = np.concatenate(forward, axis=1)
     back_table = np.stack([np.concatenate(b, axis=0) for b in backward])
-    row_sine = sine[:points, :points].copy()
+    row_sine, lag_sine = sine[:points, :points].copy(), 2.0 * sine[:points, :points]
+    row_cosine, lag_cosine = cosine[:points, :points], 2.0 * cosine[:points, :points]
     row_sine[0] = cosine[points, :points]
-    row_table = np.concatenate([cosine[:points, :points], row_sine], axis=0)
-    lag_cosine, lag_sine = 2.0 * cosine[:, :points], 2.0 * sine[:, :points]
     lag_cosine[:, 0] = 1.0
-    lag_sine[:, 0] = cosine[:, points]
-    lag_table = np.concatenate([lag_cosine, lag_sine], axis=1)
+    lag_sine[:, 0] = cosine[:points, points]
+
+
+    def woven(a, b):
+        both = np.stack([a.reshape(-1, BLOCK, points), b.reshape(-1, BLOCK, points)], axis=1)
+        return both.reshape(points, points)
+
+    row_table = np.stack([woven(row_cosine[i::2], row_sine[i::2]) for i in range(2)])
+    lag_table = np.stack([woven(lag_cosine.T[i::2], lag_sine.T[i::2]).T for i in range(2)])
     return tuple(t.astype(jnp.bfloat16) for t in (col_table, row_table, lag_table, back_table))
 
 
@@ -261,7 +268,9 @@
     opt_in,
     opt_waves,
     sar_cols,
-    sar_rows,
+    sar_head,
+    unfolded,
+    fold_v,
     cross,
     lags,
     lag_send,
@@ -293,6 +302,7 @@
     cols = wide // 4
     points = extent // 2
     per_patch = group // patch_dev
+    block = BLOCK
     send, arrived = (send_0, send_1), (arrived_0, arrived_1)
     f32, bf = jnp.float32, jnp.bfloat16
     tile, half, band = lax.axis_index("tile"), lax.axis_index("half"), lax.axis_index("band")
@@ -388,7 +398,11 @@
         if to_tile == 0:
             loads[1].wait()
         samples = jnp.concatenate(
-            [sar_v[block_for(to_tile * halves + run)] for run in range(halves)], axis=0
+            [
+                sar_v[block_for(to_tile * halves + lax.rem(run + band, halves))]
+                for run in range(halves)
+            ],
+            axis=0,
         )
         spectra = jnp.dot(samples, col_v[...], preferred_element_type=f32).astype(bf)
         for to in range(parts):
@@ -425,7 +439,7 @@
     loads[3].wait()
     loads[2].wait()
     opt_spectra = [
-        jnp.dot(opt_v[patch], col_v[...], preferred_element_type=f32).astype(bf)
+        jnp.dot(opt_v[lax.rem(patch + band, patch_dev)], col_v[...], preferred_element_type=f32).astype(bf)
         for patch in range(patch_dev)
     ]
     for to in range(parts):
@@ -460,9 +474,13 @@
     sar_sends(0, 0, (0, 1))
     for to_tile in range(1, tiles):
         sar_columns(to_tile)
-        sar_sends(0, to_tile, (0, 1))
-    for to_tile in range(tiles):
-        sar_sends(1, to_tile, (0,))
+        if to_tile > 1:
+            sar_sends(0, to_tile, (0, 1))
+        else:
+            sar_sends(1, 0, (0, 1))
+            sar_sends(0, 1, (0, 1))
+    for to_tile in range(1, tiles):
+        sar_sends(1, to_tile, (0, 1))
     arrived_0[source_at] = send_0[tile * parts + part]
     arrived_1[source_at] = send_1[tile * parts + part]
     for turn in range(2):
@@ -501,118 +519,117 @@
     lane = lax.broadcasted_iota(jnp.int32, (1, wide), 1)
     inner = lax.rem(lane, side)
     real_lane = inner < cols
-    row_at = lax.broadcasted_iota(jnp.int32, (points, 1), 0)
-    sign = jnp.where(lax.rem(row_at, 2) == 0, 1.0, -1.0)
+    top = lax.broadcasted_iota(jnp.int32, (block, wide), 0) == 0
     edge_real = [((inner + part + turn) == 0) for turn in range(2)]
     edge_imag = [((jnp.abs(inner - cols) + part + turn) == 0) for turn in range(2)]
     weights = [
-        jnp.where(edge_real[turn] | edge_imag[turn], 1.0, 2.0) * float(extent)
+        jnp.where(edge_real[turn] | edge_imag[turn], 1.0, 2.0) * (0.5 * extent)
         for turn in range(2)
     ]
 
-    def turned(z, turn):
-        ahead = pltpu.roll(z, wide - cols, 1)
-        behind = pltpu.roll(z, cols, 1)
-        return jnp.where(real_lane, -ahead, behind)
-
-    opt_energy = [0.0, 0.0]
+    def swapped(z):
+        return pltpu.roll(z, side, 1)
+
+    def crossed(z):
+        return jnp.where(real_lane, pltpu.roll(z, wide - cols, 1), pltpu.roll(z, cols, 1))
+
+    def turned(z):
+        return jnp.where(real_lane, -pltpu.roll(z, wide - cols, 1), pltpu.roll(z, cols, 1))
+
+    opt_energy = [0.0] * patch_dev
+
+    def energy_of(even, odd, head, turn):
+        shifted = even.astype(f32) - jnp.where(edge_real[turn], head * (2.0 / extent), 0.0)
+        odd = odd.astype(f32)
+        total = jnp.sum(shifted * shifted + odd * odd, axis=0, keepdims=True)
+        return total * weights[turn]
 
     def optical(turn):
         whole(opt_in.at[turn], parts - 1, opt_ssem.at[turn], opt_rsem.at[turn]).wait_recv()
-        if turn == 0:
-            for to_tile in range(tiles):
-                sar_sends(1, to_tile, (1,))
-        for source in range(bands):
-            both = jnp.concatenate(
-                [opt_in[turn, run * bands + source] for run in range(halves)], axis=1
+        real, imag = edge_real[turn], edge_imag[turn]
+        pieces = [[opt_in[turn, run * bands + b] for b in range(bands)] for run in range(halves)]
+        mixed = []
+        for patch in range(patch_dev):
+            near_x, far_x = [jnp.where(low, p[patch], p[1 - patch]) for p in pieces]
+            mixed.append((near_x + far_x, near_x - far_x))
+        for parity in range(2):
+            plain = [jnp.where(imag, 0.0, m[parity]).astype(bf) for m in mixed]
+            crossed_x = [
+                jnp.where(real, 0.0, jnp.where(imag, m[parity], turned(m[parity]))).astype(bf)
+                for m in mixed
+            ]
+            rows = jnp.dot(
+                row_v[parity], jnp.concatenate(plain + crossed_x, axis=1), preferred_element_type=f32
             )
-            rows = jnp.dot(row_v[...], both, preferred_element_type=f32)
-            mean = jnp.where(
-                edge_real[turn], (rows[0:1, :wide] + rows[0:1, wide:]) / float(extent), 0.0
-            )
-            total = 0.0
-            for run in range(halves):
-                moved = both[:, run * wide : (run + 1) * wide].astype(f32) - mean
-                total = total + jnp.sum(moved * moved, axis=0, keepdims=True)
-            opt_energy[turn] = opt_energy[turn] + total * weights[turn]
             for kind in range(2):
-                at = slice(kind * points, (kind + 1) * points)
-                near_rows, far_rows = rows[at, :wide], rows[at, wide:] * sign
-                z = near_rows + far_rows
-                z_far = pltpu.roll(z, side, 1)
-                signed, signed_far = z * sign, z_far * sign
                 for patch in range(patch_dev):
-                    if patch == 0:
-                        own = jnp.where(low, z, signed_far)
-                    else:
-                        own = jnp.where(low, z_far, signed)
-                    other = jnp.where(
-                        edge_real[turn], 0.0, jnp.where(edge_imag[turn], own, turned(own, turn))
-                    )
-                    own = jnp.where(edge_imag[turn], 0.0, own)
-                    if kind == 0:
-                        own = jnp.where(edge_real[turn] & (row_at == 0), 0.0, own)
-                    opt_waves[turn, patch, source, kind] = own
-                    opt_waves[turn, patch, source, 2 + kind] = other
-
-    block = points // 4
-    top = lax.broadcasted_iota(jnp.int32, (block, 1), 0) == 0
-
-    def fold(a, b, c, d):
-        def halve(u, v):
-            return jnp.where(low, u, v) + pltpu.roll(jnp.where(low, v, u), side, 1)
-
-        u, v = halve(a, c), halve(b, d)
-        rest = jnp.where(real_lane, v, u)
-        rest = jnp.where(
-            real_lane, pltpu.roll(rest, wide - cols, 1), pltpu.roll(rest, cols, 1)
-        )
-        return jnp.where(real_lane, u, v) + rest
+                    at = (kind * patch_dev + patch) * wide
+                    opt_waves[turn, kind, patch, parity] = rows[:, at : at + wide]
+        for patch in range(patch_dev):
+            head = opt_waves[turn, 0, patch, 0, :block]
+            opt_energy[patch] = opt_energy[patch] + energy_of(*mixed[patch], head[0:1], turn)
+            opt_waves[turn, 0, patch, 0, :block] = jnp.where(real & top, 0.0, head)
+
+    tall = (2 * patch_dev * wide, wide)
+    fold_row = lax.broadcasted_iota(jnp.int32, tall, 0)
+    fold_lane = lax.broadcasted_iota(jnp.int32, tall, 1)
+    fold_v[...] = jnp.where(
+        (lax.div(fold_row, wide) == lax.div(fold_lane, cols))
+        & (lax.rem(fold_row, cols) == lax.rem(fold_lane, cols)),
+        1.0,
+        0.0,
+    ).astype(bf)
 
     def slant(turn):
         whole(arrived[turn], others, sar_ssem.at[turn], sar_rsem.at[turn]).wait_recv()
-        if turn:
-            for shift in (1, 0):
-                lag_sends(0, shift)
         for slot in range(group):
             patch, at = slot // per_patch, slot % per_patch * lines
-            for source in range(bands):
-                pieces = [
-                    arrived[turn][slot_of[run * group + slot] * bands + source]
-                    for run in range(halves)
-                ]
-                sar_cols[turn, patch, at : at + lines, source * wide : (source + 1) * wide] = (
-                    jnp.concatenate([pieces[0][:, :side], pieces[1][:, side:]], axis=1)
+            ends = []
+            for run in range(halves):
+                source = slot_of[run * group + slot] * bands
+                piece = jnp.where(
+                    low, arrived[turn][source + run], arrived[turn][source + 1 - run]
                 )
-        for patch in range(patch_dev):
-            sar_rows[turn, patch] = jnp.dot(
-                row_v[...], sar_cols[turn, patch], preferred_element_type=f32
+                if patch != run:
+                    piece = jnp.concatenate([piece[:, side:], piece[:, :side]], axis=1)
+                ends.append(piece)
+            sar_cols[turn, 0, patch, at : at + lines, :] = ends[0] + ends[1]
+            sar_cols[turn, 1, patch, at : at + lines, :] = ends[0] - ends[1]
+        for parity in range(2):
+            both = [sar_cols[turn, parity, patch] for patch in range(patch_dev)]
+            rows = jnp.dot(
+                row_v[parity], jnp.concatenate(both, axis=1), preferred_element_type=f32
             )
-        for b in range(points // block):
-            at = slice(b * block, (b + 1) * block)
-            lower = slice(points + b * block, points + (b + 1) * block)
-            sums = [[], [], [], []]
-            for patch in range(patch_dev):
-                e_re, e_im, d_lo, d_hi = 0.0, 0.0, 0.0, 0.0
-                for source in range(bands):
-                    lanes = slice(source * wide, (source + 1) * wide)
-                    yc, ys = sar_rows[turn, patch, at, lanes], sar_rows[turn, patch, lower, lanes]
-                    zc, zs, tc, ts = [opt_waves[turn, patch, source, k, at] for k in range(4)]
-                    if b == 0:
-                        zs_e = jnp.where(top, 0.0, zs)
-                        ts_e = jnp.where(top, 0.0, ts)
-                        zc_d = jnp.where(top, zs, zc)
-                        tc_d = jnp.where(top, ts, tc)
-                    else:
-                        zs_e, ts_e, zc_d, tc_d = zs, ts, zc, tc
-                    e_re = e_re + (zc * yc + zs_e * ys)
-                    e_im = e_im + (tc * yc + ts_e * ys)
-                    d_lo = d_lo + (zc_d * ys - zs_e * yc)
-                    d_hi = d_hi + (tc_d * ys - ts_e * yc)
-                for k, term in enumerate((e_re, e_im, d_lo, d_hi)):
-                    sums[k].append(term)
-            cross[turn, at, :] = fold(sums[0][0], sums[1][0], sums[0][1], sums[1][1]).astype(bf)
-            cross[turn, lower, :] = fold(sums[2][0], sums[3][0], sums[2][1], sums[3][1]).astype(bf)
+            if parity == 0:
+                sar_head[turn] = rows[:8]
+            for b in range(points // 2 // block):
+                at = slice(2 * b * block, (2 * b + 1) * block)
+                lower = slice((2 * b + 1) * block, (2 * b + 2) * block)
+                sums = []
+                for patch in range(patch_dev):
+                    yc, ys = [rows[i, patch * wide : (patch + 1) * wide] for i in (at, lower)]
+                    zc, zs = [opt_waves[turn, 0, patch, parity, i] for i in (at, lower)]
+                    tc, ts = [opt_waves[turn, 1, patch, parity, i] for i in (at, lower)]
+                    zs_e, ts_e, zc_d, tc_d = zs, ts, zc, tc
+                    if b == 0 and parity == 0:
+                        zs_e, ts_e = jnp.where(top, 0.0, zs), jnp.where(top, 0.0, ts)
+                        zc_d, tc_d = jnp.where(top, zs, zc), jnp.where(top, ts, tc)
+                    sums.append(
+                        (
+                            zc * yc + zs_e * ys,
+                            tc * yc + ts_e * ys,
+                            zc_d * ys - zs_e * yc,
+                            tc_d * ys - ts_e * yc,
+                        )
+                    )
+                for patch in range(patch_dev):
+                    for k in range(2):
+                        lanes = slice((2 * patch + k) * wide, (2 * patch + k + 1) * wide)
+                        unfolded[parity, at, lanes] = sums[patch][k].astype(bf)
+                        unfolded[parity, lower, lanes] = sums[patch][2 + k].astype(bf)
+            cross[turn, parity] = jnp.dot(
+                unfolded[parity], fold_v[...], preferred_element_type=f32
+            ).astype(bf)
 
     def lag_copy(turn, peer):
         _, to_half, to_band = place(*peer)
@@ -630,14 +647,18 @@
                 lag_copy(turn, (0, shift, swap)).start()
 
     def spread(turn):
+        even, odd = [
+            jnp.dot(lag_v[parity], cross[turn, parity], preferred_element_type=f32)
+            for parity in range(2)
+        ]
+        flip = jnp.where(half == 0, -1.0, 1.0)
         for shift, to_half in ((1, other_half), (0, half)):
             at = pl.ds(pl.multiple_of(to_half * quarter, quarter), quarter)
-            values = jnp.dot(lag_v[at, :], cross[turn], preferred_element_type=f32).astype(bf)
+            values = (even + odd * flip if shift else even - odd * flip).astype(bf)
             lags[turn, at, :] = values
             for patch, piece in enumerate(pair(values[: quarter // 2], values[quarter // 2 :])):
                 lag_send[turn, to_half * bands + patch] = piece
-            if turn:
-                lag_sends(turn, shift)
+            lag_sends(turn, shift)
         lag_in[turn, part] = lag_send[turn, part]
 
     def gather(turn, shift, first):
@@ -656,27 +677,24 @@
 
     loads[4].wait()
     optical(0)
+    optical(1)
     slant(0)
     loads[6].wait()
     spread(0)
     loads[7].wait()
-    optical(1)
     slant(1)
     spread(1)
 
-    sar_energy = []
+    sar_energy = [0.0] * patch_dev
     for patch in range(patch_dev):
-        energy = 0.0
         for turn in range(2):
-            for source in range(bands):
-                lanes = slice(source * wide, (source + 1) * wide)
-                head = sar_rows[turn, patch, 0:1, lanes]
-                head = (head + pltpu.roll(head, side, 1)) / float(extent)
-                mean = jnp.where(edge_real[turn], head, 0.0)
-                moved = sar_cols[turn, patch, :, lanes].astype(f32) - mean
-                energy = energy + jnp.sum(moved * moved, axis=0, keepdims=True) * weights[turn]
-        sar_energy.append(energy)
-    opt_total = opt_energy[0] + opt_energy[1]
+            energy = energy_of(
+                sar_cols[turn, 0, patch],
+                sar_cols[turn, 1, patch],
+                sar_head[turn, 0:1, patch * wide : (patch + 1) * wide],
+                turn,
+            )
+            sar_energy[patch] = sar_energy[patch] + energy
 
     spot_copy.wait_recv()
     hits = jnp.concatenate([spot_send[...], spot_recv[...]], axis=0)
@@ -700,7 +718,7 @@
     for which, patch, ref in ((0, band, last_mine), (1, other_band, last_other)):
         mine = lax.div(lane, side) == patch
         ref[0:8, :] = jnp.zeros((8, wide), f32)
-        ref[0:1, :] = jnp.where(mine, opt_total, 0.0)
+        ref[0:1, :] = jnp.where(patch == 0, opt_energy[0], opt_energy[1])
         ref[1:2, :] = jnp.where(patch == 0, sar_energy[0], sar_energy[1])
         value = jnp.where(mine, found[which * peak_count : (which + 1) * peak_count], 0.0)
         ref[8 : 8 + peak_count, :] = jnp.broadcast_to(
@@ -779,8 +797,8 @@
             vmem((group, lines, extent), bf),
             vmem((patch_dev, quarter, extent), bf),
             vmem((extent, extent), bf),
-            vmem((extent, points), bf),
-            vmem((extent, extent), bf),
+            vmem((2, points, points), bf),
+            vmem((2, points, points), bf),
             vmem((2, points, extent), bf),
             vmem((tiles * parts, lines, wide), bf),
             vmem((tiles * parts, lines, wide), bf),
@@ -788,10 +806,12 @@
             vmem((group * bands, lines, wide), bf),
             vmem((2, parts, quarter, wide), bf),
             vmem((2, parts, quarter, wide), bf),
-            vmem((2, patch_dev, bands, 4, points, wide), f32),
-            vmem((2, patch_dev, points, bands * wide), bf),
-            vmem((2, patch_dev, extent, bands * wide), f32),
-            vmem((2, extent, wide), bf),
+            vmem((2, 2, patch_dev, 2, points, wide), f32),
+            vmem((2, 2, patch_dev, points, wide), bf),
+            vmem((2, 8, patch_dev * wide), f32),
+            vmem((2, points, 2 * patch_dev * wide), bf),
+            vmem((2 * patch_dev * wide, wide), bf),
+            vmem((2, 2, points, wide), bf),
             vmem((2, extent, wide), bf),
             vmem((2, parts, quarter // 2, wide), bf),
             vmem((2, parts, quarter // 2, wide), bf),

time: 26.3 us -> 25.1 us (0.954)
  the two profiles are of different devices: /device:TPU:0 before, /device:TPU:13 now
where the time goes in v2:
time: 25.1 us; the launch traced here: 24.9 us
  Pallas kernels  24.3 us (97%)
  between operations  0.64 us (3%)
    pallas_call x1, Pallas kernels, fused(): pl.pallas_call(functools.partial(kernel, sizes), out_shape=(jax.ShapeDtyp...  22.9 us
    pallas_call x1, Pallas kernels, fused(): pl.pallas_call(functools.partial(finish, bands, pieces), out_shape=(jax.S...  1.43 us

profile of v2, /device:TPU:13, one launch (start us, length us, event | category | flops | bytes accessed | tf_op | source)
XLA Modules:
  0.0 24.9 jit_solution(14725476157640171805)
XLA Ops:
  0.6 22.9 %shard_map.95 = (f32[1,256,512]{2,1,0:T(8,128)S(1)}, f32[16,128]{1,0:T(8,128)S(1)}) custom-call(s32[64]{0:T(128)} %dest_hbm.1, s32[1,2,8]{2,1,0:T(2,128)} %peaks_hbm.1, bf16[8,64,512]{2,1,0:T(8,128)(2,1)} %bitcast.2, bf16[2,256,512]{2,1,0:T(8,128)(2,1)} %bitcast.3, bf16[512,512]{1,0:T(8,128)(2,1)} %constant.8.clone.col_hbm, ...), custom_call_target="tpu_custom_call" | custom-call | tf_op jit(solution)/shard_map/pallas_call | solution.py:786
  23.5 1.4 %shard_map.96 = (f32[1,256,512]{2,1,0:T(8,128)}, f32[1,8]{1,0:T(1,128)}) custom-call(f32[1,256,512]{2,1,0:T(8,128)S(1)} %get-tuple-element.4.surface_ref, f32[16,128]{1,0:T(8,128)S(1)} %get-tuple-element.5.total_ref), custom_call_target="tpu_custom_call" | custom-call | tf_op jit(solution)/shard_map/pallas_call | solution.py:853

commit v3 on v2

--- a/solution.py
+++ b/solution.py
@@ -251,7 +251,7 @@
     lag_hbm,
     back_hbm,
     surface_ref,
-    total_ref,
+    peak_ref,
     dest_ref,
     peaks_ref,
     sar_v,
@@ -272,7 +272,9 @@
     unfolded,
     fold_v,
     cross,
-    lags,
+    spot_rows,
+    waves,
+    picked,
     lag_send,
     lag_in,
     spot_send,
@@ -648,23 +650,29 @@
 
     def spread(turn):
         even, odd = [
-            jnp.dot(lag_v[parity], cross[turn, parity], preferred_element_type=f32)
+            jnp.dot(
+                jnp.concatenate([lag_v[parity], spot_rows[parity]], axis=0),
+                cross[turn, parity],
+                preferred_element_type=f32,
+            )
             for parity in range(2)
         ]
+        picked[turn] = even[points:] + odd[points:]
+        even, odd = even[:points], odd[:points]
         flip = jnp.where(half == 0, -1.0, 1.0)
         for shift, to_half in ((1, other_half), (0, half)):
-            at = pl.ds(pl.multiple_of(to_half * quarter, quarter), quarter)
             values = (even + odd * flip if shift else even - odd * flip).astype(bf)
-            lags[turn, at, :] = values
             for patch, piece in enumerate(pair(values[: quarter // 2], values[quarter // 2 :])):
                 lag_send[turn, to_half * bands + patch] = piece
             lag_sends(turn, shift)
         lag_in[turn, part] = lag_send[turn, part]
 
-    def gather(turn, shift, first):
+    def gather(turn, shift, first=False, last=False):
         from_half = lax.rem(half + shift, halves)
         count = bands if shift else bands - 1
         whole(lag_in.at[turn], count, lag_ssem.at[turn], lag_rsem.at[turn, shift]).wait_recv()
+        if last:
+            whole(last_in, parts - 1, last_ssem, last_rsem).wait_recv()
         upper, lower = pair(*[lag_in[turn, from_half * bands + b] for b in range(bands)])
         table = back_v[turn, pl.ds(pl.multiple_of(from_half * wide, wide), wide), :]
         values = jnp.dot(
@@ -672,16 +680,50 @@
         )
         if first:
             surface_ref[0] = values
+        elif last:
+            surface_ref[0] = (surface_ref[0] + values) * norm()
         else:
             surface_ref[0] = surface_ref[0] + values
 
+    pixels = extent * extent
+
+    def norm():
+        total = last_in[0]
+        for i in range(1, parts):
+            total = total + last_in[i]
+        energies = jnp.sum(total[0:8], axis=1, keepdims=True) / (float(pixels) * bands * pixels)
+        energies = energies + EPSILON
+        scale = lax.rsqrt(bands * pixels * energies[0:1] * energies[1:2]) / pixels
+        at = lax.broadcasted_iota(jnp.int32, (peak_count, wide), 1)
+        rank = lax.broadcasted_iota(jnp.int32, (peak_count, wide), 0)
+        row = jnp.where(at == rank, total[8 : 8 + peak_count], 0.0)
+        peak_ref[...] = (jnp.sum(row, axis=0, keepdims=True) * scale)[:, :peak_count]
+        return scale
+
     loads[4].wait()
+    loads[6].wait()
+    loads[7].wait()
+    spot_copy.wait_recv()
+    spots_all = jnp.concatenate([spot_send[:peak_count], spot_recv[:peak_count]], axis=0)
+    lags_all = jnp.concatenate([spot_send[peak_count:], spot_recv[peak_count:]], axis=0)
+    upper_spots, lower_spots = spots_all[:, :points], spots_all[:, points:]
+    for parity in range(2):
+        spots_now = upper_spots + lower_spots if parity == 0 else upper_spots - lower_spots
+        spot_rows[parity] = jnp.dot(
+            spots_now, lag_v[parity], preferred_element_type=f32
+        ).astype(bf)
+    for turn in range(2):
+        rows_back = back_v[turn, pl.ds(pl.multiple_of(part * side, side), side), :]
+        waves[turn] = lax.dot_general(
+            lags_all,
+            jnp.concatenate([rows_back, rows_back], axis=0),
+            (((1,), (1,)), ((), ())),
+            preferred_element_type=f32,
+        )
     optical(0)
     optical(1)
     slant(0)
-    loads[6].wait()
     spread(0)
-    loads[7].wait()
     slant(1)
     spread(1)
 
@@ -696,25 +738,7 @@
             )
             sar_energy[patch] = sar_energy[patch] + energy
 
-    spot_copy.wait_recv()
-    hits = jnp.concatenate([spot_send[...], spot_recv[...]], axis=0)
-    found = 0.0
-    for turn in range(2):
-        picked = jnp.dot(hits, lags[turn], preferred_element_type=f32)
-        rows_back = back_v[turn, pl.ds(pl.multiple_of(part * side, side), side), :]
-        waves = lax.dot_general(
-            hits,
-            jnp.concatenate([rows_back, rows_back], axis=0),
-            (((1,), (1,)), ((), ())),
-            preferred_element_type=f32,
-        )
-        found = found + jnp.concatenate(
-            [
-                picked[:peak_count] * waves[peak_count : 2 * peak_count],
-                picked[2 * peak_count : 3 * peak_count] * waves[3 * peak_count :],
-            ],
-            axis=0,
-        )
+    found = picked[0] * waves[0] + picked[1] * waves[1]
     for which, patch, ref in ((0, band, last_mine), (1, other_band, last_other)):
         mine = lax.div(lane, side) == patch
         ref[0:8, :] = jnp.zeros((8, wide), f32)
@@ -729,13 +753,11 @@
             last_other if peer[2] else last_mine, last_in.at[part], last_ssem, last_rsem, peer
         ).start()
 
-    gather(0, 0, True)
-    gather(1, 0, False)
-    gather(0, 1, False)
-    gather(1, 1, False)
-    whole(last_in, parts - 1, last_ssem, last_rsem).wait_recv()
     last_in[part] = last_mine[...]
-    total_ref[...] = sum(last_in[i] for i in range(1, parts)) + last_in[0]
+    gather(0, 0, first=True)
+    gather(1, 0)
+    gather(0, 1)
+    gather(1, 1, last=True)
     for turn in range(2):
         whole(send[turn], others, sar_ssem.at[turn], sar_rsem.at[turn]).wait_send()
         whole(opt_in.at[turn], parts - 1, opt_ssem.at[turn], opt_rsem.at[turn]).wait_send()
@@ -744,27 +766,13 @@
     spot_copy.wait_send()
 
 
-def finish(bands, pieces, surface_ref, total_ref, out_ref, peak_ref, scaled, sem):
-    _, lines, extent = surface_ref.shape
-    pixels = extent * extent
-    peak_count = peak_ref.shape[1]
-    width = total_ref.shape[1]
-    o_all = jnp.sum(total_ref[0:1, :], axis=1, keepdims=True) / (float(pixels) * bands * pixels)
-    s_all = jnp.sum(total_ref[1:2, :], axis=1, keepdims=True) / (float(pixels) * bands * pixels)
-    norm = lax.rsqrt(bands * pixels * (o_all + EPSILON) * (s_all + EPSILON)) / pixels
-    part = lines // pieces
-    copies = []
-    for i in range(pieces):
-        at = pl.ds(i * part, part)
-        scaled[at, :] = surface_ref[0, at, :] * norm
-        copy = pltpu.make_async_copy(scaled.at[at], out_ref.at[0, at], sem.at[i])
+def finish(surface_ref, peak_in, out_ref, peak_ref, sem):
+    copies = [
+        pltpu.make_async_copy(a, b, sem.at[i])
+        for i, (a, b) in enumerate([(surface_ref, out_ref), (peak_in, peak_ref)])
+    ]
+    for copy in copies:
         copy.start()
-        copies.append(copy)
-    values = total_ref[8 : 8 + peak_count, :] * norm
-    lane = lax.broadcasted_iota(jnp.int32, (peak_count, width), 1)
-    rank = lax.broadcasted_iota(jnp.int32, (peak_count, width), 0)
-    row = jnp.sum(jnp.where(lane == rank, values, 0.0), axis=0, keepdims=True)
-    peak_ref[...] = row[:, :peak_count]
     for copy in copies:
         copy.wait()
 
@@ -783,11 +791,11 @@
     bf, f32 = jnp.bfloat16, jnp.float32
     vmem = pltpu.VMEM
     dma = pltpu.SemaphoreType.DMA
-    raw, totals = pl.pallas_call(
+    raw, values = pl.pallas_call(
         functools.partial(kernel, sizes),
         out_shape=(
             jax.ShapeDtypeStruct((1, quarter, extent), f32),
-            jax.ShapeDtypeStruct((8 + peak_count, wide), f32),
+            jax.ShapeDtypeStruct((1, peak_count), f32),
         ),
         in_specs=[pl.BlockSpec(memory_space=pltpu.HBM)] * 8,
         out_specs=(pl.BlockSpec(memory_space=pltpu.VMEM), pl.BlockSpec(memory_space=pltpu.VMEM)),
@@ -812,7 +820,9 @@
             vmem((2, points, 2 * patch_dev * wide), bf),
             vmem((2 * patch_dev * wide, wide), bf),
             vmem((2, 2, points, wide), bf),
-            vmem((2, extent, wide), bf),
+            vmem((2, 2 * peak_count, points), bf),
+            vmem((2, 2 * peak_count, wide), f32),
+            vmem((2, 2 * peak_count, wide), f32),
             vmem((2, parts, quarter // 2, wide), bf),
             vmem((2, parts, quarter // 2, wide), bf),
             vmem((2 * peak_count, extent), bf),
@@ -849,17 +859,16 @@
             )
         ]
     )
-    pieces = 4
     return pl.pallas_call(
-        functools.partial(finish, bands, pieces),
+        finish,
         out_shape=(
             jax.ShapeDtypeStruct((1, quarter, extent), f32),
             jax.ShapeDtypeStruct((1, peak_count), f32),
         ),
         in_specs=[pl.BlockSpec(memory_space=pltpu.VMEM)] * 2,
-        out_specs=(pl.BlockSpec(memory_space=pltpu.HBM), pl.BlockSpec(memory_space=pltpu.VMEM)),
-        scratch_shapes=[vmem((quarter, extent), f32), dma((pieces,))],
-    )(*[pltpu.with_memory_space_constraint(x, pltpu.VMEM) for x in (raw, totals)])
+        out_specs=(pl.BlockSpec(memory_space=pltpu.HBM), pl.BlockSpec(memory_space=pltpu.HBM)),
+        scratch_shapes=[dma((2,))],
+    )(*[pltpu.with_memory_space_constraint(x, pltpu.VMEM) for x in (raw, values)])
 
 
 def fits(mesh, optical, sar, peaks):

time: 25.1 us -> 24.6 us (0.980)
  Pallas kernels: 24.3 us -> 23.8 us
    pallas_call x1, Pallas kernels: 1.43 us -> 0.81 us  [fused(): pl.pallas_call(finish, out_shape=(jax.ShapeDtypeStruct((1, quarter, exten...]
where the time goes in v3:
time: 24.6 us; the launch traced here: 24.5 us
  Pallas kernels  23.8 us (97%)
  between operations  0.64 us (3%)
    pallas_call x1, Pallas kernels, fused(): pl.pallas_call(functools.partial(kernel, sizes), out_shape=(jax.ShapeDtyp...  23 us
    pallas_call x1, Pallas kernels, fused(): pl.pallas_call(finish, out_shape=(jax.ShapeDtypeStruct((1, quarter, exten...  0.81 us

profile of v3, /device:TPU:13, one launch (start us, length us, event | category | flops | bytes accessed | tf_op | source)
XLA Modules:
  0.0 24.5 jit_solution(1223058973127270514)
XLA Ops:
  0.6 23.0 %shard_map.95 = (f32[1,256,512]{2,1,0:T(8,128)S(1)}, f32[1,8]{1,0:T(1,128)S(1)}) custom-call(s32[64]{0:T(128)} %dest_hbm.1, s32[1,2,8]{2,1,0:T(2,128)} %peaks_hbm.1, bf16[8,64,512]{2,1,0:T(8,128)(2,1)} %bitcast.2, bf16[2,256,512]{2,1,0:T(8,128)(2,1)} %bitcast.3, bf16[512,512]{1,0:T(8,128)(2,1)} %constant.8.clone.col_hbm, ...), custom_call_target="tpu_custom_call" | custom-call | tf_op jit(solution)/shard_map/pallas_call | solution.py:794
  23.7 0.8 %shard_map.96 = (f32[1,256,512]{2,1,0:T(8,128)}, f32[1,8]{1,0:T(1,128)}) custom-call(f32[1,256,512]{2,1,0:T(8,128)S(1)} %get-tuple-element.4.surface_ref, f32[1,8]{1,0:T(1,128)S(1)} %get-tuple-element.5.peak_in), custom_call_target="tpu_custom_call" | custom-call | tf_op jit(solution)/shard_map/pallas_call | solution.py:862

commit v4 on v3

--- a/solution.py
+++ b/solution.py
@@ -268,9 +268,6 @@
     opt_in,
     opt_waves,
     sar_cols,
-    sar_head,
-    unfolded,
-    fold_v,
     cross,
     spot_rows,
     waves,
@@ -473,16 +470,16 @@
     def _():
         pl.semaphore_wait(far_sem, 1)
 
-    sar_sends(0, 0, (0, 1))
+    sar_sends(0, 0, (1, 0))
     for to_tile in range(1, tiles):
         sar_columns(to_tile)
         if to_tile > 1:
-            sar_sends(0, to_tile, (0, 1))
+            sar_sends(0, to_tile, (1, 0))
         else:
-            sar_sends(1, 0, (0, 1))
-            sar_sends(0, 1, (0, 1))
+            sar_sends(1, 0, (1, 0))
+            sar_sends(0, 1, (1, 0))
     for to_tile in range(1, tiles):
-        sar_sends(1, to_tile, (0, 1))
+        sar_sends(1, to_tile, (1, 0))
     arrived_0[source_at] = send_0[tile * parts + part]
     arrived_1[source_at] = send_1[tile * parts + part]
     for turn in range(2):
@@ -572,15 +569,14 @@
             opt_energy[patch] = opt_energy[patch] + energy_of(*mixed[patch], head[0:1], turn)
             opt_waves[turn, 0, patch, 0, :block] = jnp.where(real & top, 0.0, head)
 
-    tall = (2 * patch_dev * wide, wide)
-    fold_row = lax.broadcasted_iota(jnp.int32, tall, 0)
-    fold_lane = lax.broadcasted_iota(jnp.int32, tall, 1)
-    fold_v[...] = jnp.where(
-        (lax.div(fold_row, wide) == lax.div(fold_lane, cols))
-        & (lax.rem(fold_row, cols) == lax.rem(fold_lane, cols)),
-        1.0,
-        0.0,
-    ).astype(bf)
+    def fold(a, b, c, d):
+        def halve(u, v):
+            return jnp.where(low, u, v) + swapped(jnp.where(low, v, u))
+
+        u, v = halve(a, c), halve(b, d)
+        return (jnp.where(real_lane, u, v) + crossed(jnp.where(real_lane, v, u))).astype(bf)
+
+    sar_energy = [0.0] * patch_dev
 
     def slant(turn):
         whole(arrived[turn], others, sar_ssem.at[turn], sar_rsem.at[turn]).wait_recv()
@@ -603,7 +599,14 @@
                 row_v[parity], jnp.concatenate(both, axis=1), preferred_element_type=f32
             )
             if parity == 0:
-                sar_head[turn] = rows[:8]
+                for patch in range(patch_dev):
+                    energy = energy_of(
+                        sar_cols[turn, 0, patch],
+                        sar_cols[turn, 1, patch],
+                        rows[0:1, patch * wide : (patch + 1) * wide],
+                        turn,
+                    )
+                    sar_energy[patch] = sar_energy[patch] + energy
             for b in range(points // 2 // block):
                 at = slice(2 * b * block, (2 * b + 1) * block)
                 lower = slice((2 * b + 1) * block, (2 * b + 2) * block)
@@ -624,14 +627,9 @@
                             tc_d * ys - ts_e * yc,
                         )
                     )
-                for patch in range(patch_dev):
-                    for k in range(2):
-                        lanes = slice((2 * patch + k) * wide, (2 * patch + k + 1) * wide)
-                        unfolded[parity, at, lanes] = sums[patch][k].astype(bf)
-                        unfolded[parity, lower, lanes] = sums[patch][2 + k].astype(bf)
-            cross[turn, parity] = jnp.dot(
-                unfolded[parity], fold_v[...], preferred_element_type=f32
-            ).astype(bf)
+                one, two = sums
+                cross[turn, parity, at, :] = fold(one[0], one[1], two[0], two[1])
+                cross[turn, parity, lower, :] = fold(one[2], one[3], two[2], two[3])
 
     def lag_copy(turn, peer):
         _, to_half, to_band = place(*peer)
@@ -648,17 +646,36 @@
             if shift or swap:
                 lag_copy(turn, (0, shift, swap)).start()
 
+    def send_last():
+        found = picked[0] * waves[0] + picked[1] * waves[1]
+        for which, patch, ref in ((0, band, last_mine), (1, other_band, last_other)):
+            mine = lax.div(lane, side) == patch
+            ref[0:8, :] = jnp.zeros((8, wide), f32)
+            ref[0:1, :] = jnp.where(patch == 0, opt_energy[0], opt_energy[1])
+            ref[1:2, :] = jnp.where(patch == 0, sar_energy[0], sar_energy[1])
+            value = jnp.where(mine, found[which * peak_count : (which + 1) * peak_count], 0.0)
+            ref[8 : 8 + peak_count, :] = jnp.broadcast_to(
+                jnp.sum(value, axis=1, keepdims=True), (peak_count, wide)
+            )
+        for peer in near:
+            remote(
+                last_other if peer[2] else last_mine, last_in.at[part], last_ssem, last_rsem, peer
+            ).start()
+        last_in[part] = last_mine[...]
+
     def spread(turn):
         even, odd = [
             jnp.dot(
-                jnp.concatenate([lag_v[parity], spot_rows[parity]], axis=0),
+                jnp.concatenate([spot_rows[parity], lag_v[parity]], axis=0),
                 cross[turn, parity],
                 preferred_element_type=f32,
             )
             for parity in range(2)
         ]
-        picked[turn] = even[points:] + odd[points:]
-        even, odd = even[:points], odd[:points]
+        picked[turn] = even[: 2 * peak_count] + odd[: 2 * peak_count]
+        even, odd = even[2 * peak_count :], odd[2 * peak_count :]
+        if turn:
+            send_last()
         flip = jnp.where(half == 0, -1.0, 1.0)
         for shift, to_half in ((1, other_half), (0, half)):
             values = (even + odd * flip if shift else even - odd * flip).astype(bf)
@@ -669,10 +686,11 @@
 
     def gather(turn, shift, first=False, last=False):
         from_half = lax.rem(half + shift, halves)
+        if last:
+            whole(last_in, parts - 1, last_ssem, last_rsem).wait_recv()
+            scale = norm()
         count = bands if shift else bands - 1
         whole(lag_in.at[turn], count, lag_ssem.at[turn], lag_rsem.at[turn, shift]).wait_recv()
-        if last:
-            whole(last_in, parts - 1, last_ssem, last_rsem).wait_recv()
         upper, lower = pair(*[lag_in[turn, from_half * bands + b] for b in range(bands)])
         table = back_v[turn, pl.ds(pl.multiple_of(from_half * wide, wide), wide), :]
         values = jnp.dot(
@@ -681,7 +699,7 @@
         if first:
             surface_ref[0] = values
         elif last:
-            surface_ref[0] = (surface_ref[0] + values) * norm()
+            surface_ref[0] = (surface_ref[0] + values) * scale
         else:
             surface_ref[0] = surface_ref[0] + values
 
@@ -727,33 +745,6 @@
     slant(1)
     spread(1)
 
-    sar_energy = [0.0] * patch_dev
-    for patch in range(patch_dev):
-        for turn in range(2):
-            energy = energy_of(
-                sar_cols[turn, 0, patch],
-                sar_cols[turn, 1, patch],
-                sar_head[turn, 0:1, patch * wide : (patch + 1) * wide],
-                turn,
-            )
-            sar_energy[patch] = sar_energy[patch] + energy
-
-    found = picked[0] * waves[0] + picked[1] * waves[1]
-    for which, patch, ref in ((0, band, last_mine), (1, other_band, last_other)):
-        mine = lax.div(lane, side) == patch
-        ref[0:8, :] = jnp.zeros((8, wide), f32)
-        ref[0:1, :] = jnp.where(patch == 0, opt_energy[0], opt_energy[1])
-        ref[1:2, :] = jnp.where(patch == 0, sar_energy[0], sar_energy[1])
-        value = jnp.where(mine, found[which * peak_count : (which + 1) * peak_count], 0.0)
-        ref[8 : 8 + peak_count, :] = jnp.broadcast_to(
-            jnp.sum(value, axis=1, keepdims=True), (peak_count, wide)
-        )
-    for peer in near:
-        remote(
-            last_other if peer[2] else last_mine, last_in.at[part], last_ssem, last_rsem, peer
-        ).start()
-
-    last_in[part] = last_mine[...]
     gather(0, 0, first=True)
     gather(1, 0)
     gather(0, 1)
@@ -816,9 +807,6 @@
             vmem((2, parts, quarter, wide), bf),
             vmem((2, 2, patch_dev, 2, points, wide), f32),
             vmem((2, 2, patch_dev, points, wide), bf),
-            vmem((2, 8, patch_dev * wide), f32),
-            vmem((2, points, 2 * patch_dev * wide), bf),
-            vmem((2 * patch_dev * wide, wide), bf),
             vmem((2, 2, points, wide), bf),
             vmem((2, 2 * peak_count, points), bf),
             vmem((2, 2 * peak_count, wide), f32),
@@ -881,6 +869,7 @@
         and patch_dev == 2
         and local_bands == 1
         and lines % 16 == 0
+        and mesh.shape["tile"] > 1
         and quarter * 2 == extent
         and group * lines == patch_dev * quarter
         and extent % 512 == 0

time: 24.6 us -> 24.4 us (level)
    pallas_call x1, Pallas kernels: 23 us -> 22.8 us  [fused(): pl.pallas_call(functools.partial(kernel, sizes), out_shape=(jax.ShapeDtyp...]
where the time goes in v4:
time: 24.4 us; the launch traced here: 24.2 us
  Pallas kernels  23.6 us (97%)
  between operations  0.64 us (3%)
    pallas_call x1, Pallas kernels, fused(): pl.pallas_call(functools.partial(kernel, sizes), out_shape=(jax.ShapeDtyp...  22.8 us
    pallas_call x1, Pallas kernels, fused(): pl.pallas_call(finish, out_shape=(jax.ShapeDtypeStruct((1, quarter, exten...  0.81 us

profile of v4, /device:TPU:13, one launch (start us, length us, event | category | flops | bytes accessed | tf_op | source)
XLA Modules:
  0.0 24.2 jit_solution(1402003203136166608)
XLA Ops:
  0.6 22.8 %shard_map.95 = (f32[1,256,512]{2,1,0:T(8,128)S(1)}, f32[1,8]{1,0:T(1,128)S(1)}) custom-call(s32[64]{0:T(128)} %dest_hbm.1, s32[1,2,8]{2,1,0:T(2,128)} %peaks_hbm.1, bf16[8,64,512]{2,1,0:T(8,128)(2,1)} %bitcast.2, bf16[2,256,512]{2,1,0:T(8,128)(2,1)} %bitcast.3, bf16[512,512]{1,0:T(8,128)(2,1)} %constant.8.clone.col_hbm, ...), custom_call_target="tpu_custom_call" | custom-call | tf_op jit(solution)/shard_map/pallas_call | solution.py:785
  23.4 0.8 %shard_map.96 = (f32[1,256,512]{2,1,0:T(8,128)}, f32[1,8]{1,0:T(1,128)}) custom-call(f32[1,256,512]{2,1,0:T(8,128)S(1)} %get-tuple-element.4.surface_ref, f32[1,8]{1,0:T(1,128)S(1)} %get-tuple-element.5.peak_in), custom_call_target="tpu_custom_call" | custom-call | tf_op jit(solution)/shard_map/pallas_call | solution.py:850

commit v5 on v4

--- a/solution.py
+++ b/solution.py
@@ -413,13 +413,12 @@
     def sar_sends(turn, to_tile, shifts):
         for shift in shifts:
             to_half = lax.rem(half + shift, halves)
-            for swap in range(bands):
-                to_band = lax.rem(band + swap, bands)
-                copy = sar_copy(turn, to_tile, to_half, to_band)
-                if shift or swap:
+            for to_band in reversed(range(bands)):
+                copy = sar_copy(turn, to_tile, to_half, jnp.int32(to_band))
+                if shift:
                     copy.start()
                 else:
-                    pl.when(tile != to_tile)(copy.start)
+                    pl.when((tile != to_tile) | (band != to_band))(copy.start)
 
     def opt_copy(turn, peer):
         _, to_half, to_band = place(*peer)
@@ -431,9 +430,13 @@
             peer,
         )
 
+    def to_core(copy_of, turn, to_band):
+        return copy_of(turn, (0, 1, lax.rem(to_band + bands - band, bands)))
+
     def opt_sends(turn):
-        for peer in near:
-            opt_copy(turn, peer).start()
+        for to_band in reversed(range(bands)):
+            to_core(opt_copy, turn, to_band).start()
+        opt_copy(turn, (0, 0, 1)).start()
 
     loads[3].wait()
     loads[2].wait()

time: 24.4 us -> 24 us (0.984)
  Pallas kernels: 23.6 us -> 23.2 us
    pallas_call x1, Pallas kernels: 22.8 us -> 22.4 us  [fused(): pl.pallas_call(functools.partial(kernel, sizes), out_shape=(jax.ShapeDtyp...]
where the time goes in v5:
time: 24 us; the launch traced here: 23.9 us
  Pallas kernels  23.2 us (97%)
  between operations  0.64 us (3%)
    pallas_call x1, Pallas kernels, fused(): pl.pallas_call(functools.partial(kernel, sizes), out_shape=(jax.ShapeDtyp...  22.4 us
    pallas_call x1, Pallas kernels, fused(): pl.pallas_call(finish, out_shape=(jax.ShapeDtypeStruct((1, quarter, exten...  0.81 us

profile of v5, /device:TPU:13, one launch (start us, length us, event | category | flops | bytes accessed | tf_op | source)
XLA Modules:
  0.0 23.9 jit_solution(9966709353299374184)
XLA Ops:
  0.6 22.4 %shard_map.95 = (f32[1,256,512]{2,1,0:T(8,128)S(1)}, f32[1,8]{1,0:T(1,128)S(1)}) custom-call(s32[64]{0:T(128)} %dest_hbm.1, s32[1,2,8]{2,1,0:T(2,128)} %peaks_hbm.1, bf16[8,64,512]{2,1,0:T(8,128)(2,1)} %bitcast.2, bf16[2,256,512]{2,1,0:T(8,128)(2,1)} %bitcast.3, bf16[512,512]{1,0:T(8,128)(2,1)} %constant.8.clone.col_hbm, ...), custom_call_target="tpu_custom_call" | custom-call | tf_op jit(solution)/shard_map/pallas_call | solution.py:788
  23.0 0.8 %shard_map.96 = (f32[1,256,512]{2,1,0:T(8,128)}, f32[1,8]{1,0:T(1,128)}) custom-call(f32[1,256,512]{2,1,0:T(8,128)S(1)} %get-tuple-element.4.surface_ref, f32[1,8]{1,0:T(1,128)S(1)} %get-tuple-element.5.peak_in), custom_call_target="tpu_custom_call" | custom-call | tf_op jit(solution)/shard_map/pallas_call | solution.py:853

commit v6 on v5

--- a/solution.py
+++ b/solution.py
@@ -474,15 +474,16 @@
         pl.semaphore_wait(far_sem, 1)
 
     sar_sends(0, 0, (1, 0))
-    for to_tile in range(1, tiles):
-        sar_columns(to_tile)
-        if to_tile > 1:
-            sar_sends(0, to_tile, (1, 0))
-        else:
-            sar_sends(1, 0, (1, 0))
-            sar_sends(0, 1, (1, 0))
-    for to_tile in range(1, tiles):
-        sar_sends(1, to_tile, (1, 0))
+    sar_sends(1, 0, (1, 0))
+    sar_columns(1)
+    sar_sends(0, 1, (1, 0))
+    sar_columns(3)
+    sar_sends(0, 3, (1, 0))
+    sar_columns(2)
+    sar_sends(0, 2, (1, 0))
+    sar_sends(1, 1, (1, 0))
+    sar_sends(1, 3, (1, 0))
+    sar_sends(1, 2, (1, 0))
     arrived_0[source_at] = send_0[tile * parts + part]
     arrived_1[source_at] = send_1[tile * parts + part]
     for turn in range(2):

time: 24 us -> 24 us (level)
  no operation moved by 1% of the time
where the time goes in v6:
time: 24 us; the launch traced here: 23.9 us
  Pallas kernels  23.2 us (97%)
  between operations  0.64 us (3%)
    pallas_call x1, Pallas kernels, fused(): pl.pallas_call(functools.partial(kernel, sizes), out_shape=(jax.ShapeDtyp...  22.4 us
    pallas_call x1, Pallas kernels, fused(): pl.pallas_call(finish, out_shape=(jax.ShapeDtypeStruct((1, quarter, exten...  0.81 us

profile of v6, /device:TPU:13, one launch (start us, length us, event | category | flops | bytes accessed | tf_op | source)
XLA Modules:
  0.0 23.9 jit_solution(10001625668915816170)
XLA Ops:
  0.6 22.4 %shard_map.95 = (f32[1,256,512]{2,1,0:T(8,128)S(1)}, f32[1,8]{1,0:T(1,128)S(1)}) custom-call(s32[64]{0:T(128)} %dest_hbm.1, s32[1,2,8]{2,1,0:T(2,128)} %peaks_hbm.1, bf16[8,64,512]{2,1,0:T(8,128)(2,1)} %bitcast.2, bf16[2,256,512]{2,1,0:T(8,128)(2,1)} %bitcast.3, bf16[512,512]{1,0:T(8,128)(2,1)} %constant.8.clone.col_hbm, ...), custom_call_target="tpu_custom_call" | custom-call | tf_op jit(solution)/shard_map/pallas_call | solution.py:789
  23.0 0.8 %shard_map.96 = (f32[1,256,512]{2,1,0:T(8,128)}, f32[1,8]{1,0:T(1,128)}) custom-call(f32[1,256,512]{2,1,0:T(8,128)S(1)} %get-tuple-element.4.surface_ref, f32[1,8]{1,0:T(1,128)S(1)} %get-tuple-element.5.peak_in), custom_call_target="tpu_custom_call" | custom-call | tf_op jit(solution)/shard_map/pallas_call | solution.py:854
